TPU v7x, 16 devices: a whole 2x2x2 slice. The times are simulated.
16 devices in a mesh: rep: 1, r: 2 (over z), s: 8 (over x, y, core).
Axes of the slice: x: 2, y: 2, z: 2, core: 2. Of those that a mesh axis runs over, the one named last changes fastest.
Arguments:
- x: bfloat16 [16, 2048, 1280], P(('rep', 'r', 's'))
- dy: bfloat16 [16, 2048, 1280], P(('rep', 'r', 's'))
- w_gate: bfloat16 [2, 1280, 3072], P(None, 's')
- w_up: bfloat16 [2, 1280, 3072], P(None, 's')
- w_down: bfloat16 [2, 3072, 1280], P(None, 's')
Outputs:
- output 1: bfloat16 [16, 2048, 1280], P(('rep', 'r', 's'))
- output 2: bfloat16 [2, 1280, 3072], P('rep', 's')
- output 3: bfloat16 [2, 1280, 3072], P('rep', 's')
- output 4: bfloat16 [2, 3072, 1280], P('rep', 's')
All inputs are finite; a program needn't handle non-finite values.
Results may differ from a plain program's by a relative error of at most 0.018.
Values are sent between devices in bfloat16 or wider.
A program may use at most 2 GiB of HBM per device.

v0:
```python
import jax
import jax.numpy as jnp
from jax import lax
from jax.sharding import PartitionSpec as P

NAMES = ("w_gate", "w_up", "w_down")


def matmul(a, w):
    return jnp.dot(a, w, preferred_element_type=jnp.float32).astype(jnp.bfloat16)


def normed(h):
    wide = h.astype(jnp.float32)
    scale = lax.rsqrt(jnp.mean(wide**2, -1, keepdims=True) + 1e-6)
    return (wide * scale).astype(jnp.bfloat16)


def layer(h, w):
    a = normed(h)
    gate = jnp.dot(a, w["w_gate"], preferred_element_type=jnp.float32)
    up = jnp.dot(a, w["w_up"], preferred_element_type=jnp.float32)
    return h + matmul((jax.nn.silu(gate) * up).astype(jnp.bfloat16), w["w_down"])


def solution(mesh):
    def fetched(weights, number):
        return {name: lax.all_gather(w[number], "s", axis=0, tiled=True) for name, w in zip(NAMES, weights, strict=True)}

    def summed(term):
        return lax.psum(lax.psum_scatter(term, "s", scatter_dimension=0, tiled=True), "r")

    def step(x, dy, *weights):
        layers = weights[0].shape[0]
        h, inputs = x[0], []
        for number in range(layers):
            inputs.append(h)
            h = layer(h, fetched(weights, number))
        by_h, mine = dy[0], [None] * layers
        for number in reversed(range(layers)):
            _, back = jax.vjp(lambda w, h: layer(h, w), fetched(weights, number), inputs[number])
            by_w, by_h = back(by_h)
            mine[number] = [summed(by_w[name]) for name in NAMES]
        return (by_h[None], *(jnp.stack([mine[number][i] for number in range(layers)]) for i in range(3)))

    states, cut = P(("rep", "r", "s"), None, None), P(None, "s", None)
    return jax.shard_map(
        step,
        mesh=mesh,
        in_specs=(states, states) + (cut,) * 3,
        out_specs=(states,) + (P("rep", "s", None),) * 3,
        check_vma=False,
    )
```

profile of v0, /device:TPU:0, one launch (start us, length us, event | category | flops | bytes accessed | tf_op | source)
XLA Modules:
  0.0 948.1 jit_solution(17212535457474876239)
XLA Ops:
  16.5 7.9 copy.10
  28.6 7.9 copy.9
  36.5 24.7 %all-gather.13.cloned.1.call-done = bf16[1,1280,3072]{2,1,0:T(8,128)(2,1)} async-done(((bf16[1,160,3072]{2,1,0:T(8,128)(2,1)}), bf16[1,1280,3072]{2,1,0:T(8,128)(2,1)}) %all-gather.13.cloned.1.call-update) | async-done | bytes 7864336 | tf_op jit(solution)/shard_map/all_gather | solution.py:28
  61.2 23.5 %fusion.40 = f32[2048,3072]{1,0:T(8,128)} fusion(bf16[1,1280,3072]{2,1,0:T(8,128)(2,1)} %all-gather.13.cloned.1.call-done, bf16[1,2048,1280]{1,2,0:T(8,128)(2,1)} %copy.10, f32[2048]{0:T(1024)S(1)} %fusion.79), kind=kOutput, calls=%fused_computation.65 | convolution fusion | flops 16113991680 | bytes 38281216 | tf_op jit(solution)/shard_map/dot_general | solution.py:21
  84.7 26.3 %all-gather.15.cloned.1.call-done = bf16[1,1280,3072]{2,1,0:T(8,128)(2,1)} async-done(((bf16[1,160,3072]{2,1,0:T(8,128)(2,1)}), bf16[1,1280,3072]{2,1,0:T(8,128)(2,1)}) %all-gather.15.cloned.1.call-update) | async-done | bytes 7864336 | tf_op jit(solution)/shard_map/all_gather | solution.py:28
  111.0 34.7 %multiply_convert_fusion.1 = (bf16[2048,3072]{1,0:T(8,128)(2,1)}, f32[2048,3072]{1,0:T(8,128)}) fusion(f32[2048,3072]{1,0:T(8,128)} %fusion.40, bf16[1,1280,3072]{2,1,0:T(8,128)(2,1)} %all-gather.15.cloned.1.call-done, bf16[1,2048,1280]{1,2,0:T(8,128)(2,1)} %copy.10, f32[2048]{0:T(1024)S(1)} %fusion.79), kind=kOutput, calls=%fused_computation.13 | convolution fusion | flops 16151740416 | bytes 76029952 | tf_op jit(solution)/shard_map/dot_general | solution.py:22
  145.8 15.1 %all-gather.17.cloned.1.call-done = bf16[1,3072,1280]{2,1,0:T(8,128)(2,1)} async-done(((bf16[1,384,1280]{2,1,0:T(8,128)(2,1)}), bf16[1,3072,1280]{2,1,0:T(8,128)(2,1)}) %all-gather.17.cloned.1.call-update) | async-done | bytes 7864336 | tf_op jit(solution)/shard_map/all_gather | solution.py:28
  160.9 23.6 %fusion.21 = (f32[2048]{0:T(1024)S(1)}, bf16[2048,1280]{0,1:T(8,128)(2,1)}) fusion(bf16[2048,3072]{1,0:T(8,128)(2,1)} %get-tuple-element.20, bf16[1,3072,1280]{2,1,0:T(8,128)(2,1)} %all-gather.17.cloned.1.call-done, bf16[1,2048,1280]{1,2,0:T(8,128)(2,1)} %copy.10), kind=kOutput, calls=%fused_computation.46 | convolution fusion | flops 16119232512 | bytes 30941184 | tf_op jit(solution)/shard_map/dot_general | solution.py:10
  185.1 25.5 %all-gather.21.cloned.1.call-done = bf16[1,3072,1280]{2,1,0:T(8,128)(2,1)} async-done(((bf16[1,384,1280]{2,1,0:T(8,128)(2,1)}), bf16[1,3072,1280]{2,1,0:T(8,128)(2,1)}) %all-gather.21.cloned.1.call-update) | async-done | bytes 7864336 | tf_op jit(solution)/shard_map/all_gather | solution.py:28
  210.6 22.8 %convolution_convert_fusion.2 = bf16[2048,3072]{1,0:T(8,128)(2,1)} fusion(bf16[1,3072,1280]{2,1,0:T(8,128)(2,1)} %all-gather.21.cloned.1.call-done, bf16[1,2048,1280]{2,1,0:T(8,128)(2,1)} %param.6), kind=kOutput, calls=%fused_computation.36 | convolution fusion | flops 16112418816 | bytes 25690112 | tf_op jit(solution)/shard_map/transpose(jvp())/dot_general | solution.py:10
  233.4 27.4 %all-gather.23.cloned.1.call-done = bf16[1,1280,3072]{2,1,0:T(8,128)(2,1)} async-done(((bf16[1,160,3072]{2,1,0:T(8,128)(2,1)}), bf16[1,1280,3072]{2,1,0:T(8,128)(2,1)}) %all-gather.23.cloned.1.call-update) | async-done | bytes 7864336 | tf_op jit(solution)/shard_map/all_gather | solution.py:28
  260.8 23.6 %fusion.24 = f32[2048,3072]{1,0:T(8,128)} fusion(bf16[1,1280,3072]{2,1,0:T(8,128)(2,1)} %all-gather.23.cloned.1.call-done, bf16[2048,1280]{0,1:T(8,128)(2,1)} %get-tuple-element.23, f32[2048]{0:T(1024)S(1)} %fusion.80), kind=kOutput, calls=%fused_computation.49 | convolution fusion | flops 16113991680 | bytes 38281216 | tf_op jit(solution)/shard_map/jvp()/dot_general | solution.py:22
  284.4 26.7 %all-gather.19.cloned.1.call-done = bf16[1,1280,3072]{2,1,0:T(8,128)(2,1)} async-done(((bf16[1,160,3072]{2,1,0:T(8,128)(2,1)}), bf16[1,1280,3072]{2,1,0:T(8,128)(2,1)}) %all-gather.19.cloned.1.call-update) | async-done | bytes 7864336 | tf_op jit(solution)/shard_map/all_gather | solution.py:28
  311.1 38.7 %fusion.1 = (bf16[2048,3072]{1,0:T(8,128)(2,1)}, f32[2048,3072]{1,0:T(8,128)}) fusion(f32[2048,3072]{1,0:T(8,128)} %fusion.24, bf16[2048,3072]{1,0:T(8,128)(2,1)} %convolution_convert_fusion.2, bf16[1,1280,3072]{2,1,0:T(8,128)(2,1)} %all-gather.19.cloned.1.call-done, bf16[2048,1280]{0,1:T(8,128)(2,1)} %get-tuple-element.23, f32[2048]{0:T(1024)S(1)} %fusion.80), kind=kOutput, calls=%fused_computation.7 | convolution fusion | flops 16189489152 | bytes 88612864 | tf_op jit(solution)/shard_map/jvp()/dot_general | solution.py:21
  349.8 28.7 %fusion.11 = bf16[3072,1280]{1,0:T(8,128)(2,1)} fusion(f32[2048,3072]{1,0:T(8,128)} %fusion.24, bf16[1,2048,1280]{2,1,0:T(8,128)(2,1)} %param.6, f32[2048,3072]{1,0:T(8,128)} %get-tuple-element.25), kind=kOutput, calls=%fused_computation.32 | convolution fusion | flops 16147808256 | bytes 63438848 | tf_op jit(solution)/shard_map/transpose(jvp())/dot_general | solution.py:10
  378.6 21.8 %fusion.48 = bf16[2048,1280]{0,1:T(8,128)(2,1)S(1)} fusion(bf16[2048,3072]{1,0:T(8,128)(2,1)} %get-tuple-element.24, bf16[1,1280,3072]{2,1,0:T(8,128)(2,1)} %all-gather.19.cloned.1.call-done), kind=kOutput, calls=%fused_computation.69 | convolution fusion | flops 16106127360 | bytes 25690112 | tf_op jit(solution)/shard_map/transpose(jvp())/dot_general | solution.py:21
  400.4 26.2 %fusion.23 = (f32[2048]{0:T(1024)S(1)}, bf16[2048,1280]{0,1:T(8,128)(2,1)}) fusion(bf16[2048,1280]{0,1:T(8,128)(2,1)S(1)} %bitcast.93, bf16[2048,1280]{0,1:T(8,128)(2,1)S(1)} %fusion.48, bf16[1,1280,3072]{2,1,0:T(8,128)(2,1)} %all-gather.23.cloned.1.call-done, bf16[2048,3072]{1,0:T(8,128)(2,1)} %convolution_convert_fusion.2, f32[2048,3072]{1,0:T(8,128)} %get-tuple-element.25), kind=kOutput, calls=%fused_computation.48 | convolution fusion | flops 16159602688 | bytes 61349888 | tf_op jit(solution)/shard_map/transpose(jvp())/dot_general | solution.py:22
  426.6 12.3 %fusion.68 = bf16[2048,1280]{0,1:T(8,128)(2,1)} fusion(bf16[2048,1280]{0,1:T(8,128)(2,1)} %get-tuple-element.23, bf16[2048,1280]{0,1:T(8,128)(2,1)} %get-tuple-element.27, bf16[1,2048,1280]{1,2,0:T(8,128)(2,1)} %copy.9, f32[2048]{0:T(1024)S(1)} %multiply_multiply_fusion.1, f32[2048]{0:T(1024)S(1)} %copy-done.6), kind=kLoop, calls=%fused_computation.77 | loop fusion | flops 18350080 | bytes 20987904 | tf_op jit(solution)/shard_map/transpose(jvp())/add_any | solution.py:14
  438.9 22.4 %convolution_convert_fusion = bf16[3072,1280]{1,0:T(8,128)(2,1)} fusion(bf16[2048,3072]{1,0:T(8,128)(2,1)} %get-tuple-element.20, bf16[2048,1280]{0,1:T(8,128)(2,1)} %fusion.68), kind=kOutput, calls=%fused_computation.31 | convolution fusion | flops 16110059520 | bytes 25690112 | tf_op jit(solution)/shard_map/transpose(jvp())/dot_general | solution.py:10
  461.4 38.6 %fusion.3 = (bf16[2048,3072]{1,0:T(8,128)(2,1)}, bf16[2048,3072]{1,0:T(8,128)(2,1)}) fusion(f32[2048,3072]{1,0:T(8,128)} %fusion.40, f32[2048,3072]{1,0:T(8,128)} %get-tuple-element.21, bf16[2048,1280]{0,1:T(8,128)(2,1)} %fusion.68, bf16[1,3072,1280]{2,1,0:T(8,128)(2,1)} %all-gather.17.cloned.1.call-done), kind=kOutput, calls=%fused_computation.9 | convolution fusion | flops 16187916288 | bytes 88604672 | tf_op jit(solution)/shard_map/transpose(jvp())/dot_general | solution.py:10
  500.0 25.1 %fusion.12 = bf16[1280,3072]{1,0:T(8,128)(2,1)} fusion(bf16[2048,3072]{1,0:T(8,128)(2,1)} %get-tuple-element.29, bf16[1,2048,1280]{1,2,0:T(8,128)(2,1)} %copy.10, f32[2048]{0:T(1024)S(1)} %copy-done.4, f32[2048,3072]{1,0:T(8,128)} %fusion.40), kind=kOutput, calls=%fused_computation.33 | convolution fusion | flops 16155672576 | bytes 50864128 | tf_op jit(solution)/shard_map/transpose(jvp())/dot_general | solution.py:22
  525.2 25.3 %fusion.13 = bf16[1280,3072]{1,0:T(8,128)(2,1)} fusion(bf16[2048,3072]{1,0:T(8,128)(2,1)} %convolution_convert_fusion.2, bf16[2048,1280]{0,1:T(8,128)(2,1)} %get-tuple-element.23, f32[2048]{0:T(1024)S(1)} %copy-done.7, f32[2048,3072]{1,0:T(8,128)} %get-tuple-element.25), kind=kOutput, calls=%fused_computation.34 | convolution fusion | flops 16155672576 | bytes 50864128 | tf_op jit(solution)/shard_map/transpose(jvp())/dot_general | solution.py:22
  550.5 22.2 %convolution_convert_fusion.3 = bf16[1280,3072]{1,0:T(8,128)(2,1)} fusion(bf16[2048,3072]{1,0:T(8,128)(2,1)} %get-tuple-element.24, bf16[2048,1280]{0,1:T(8,128)(2,1)} %get-tuple-element.23, f32[2048]{0:T(1024)S(1)} %copy-done.7), kind=kOutput, calls=%fused_computation.37 | convolution fusion | flops 16113991680 | bytes 25698304 | tf_op jit(solution)/shard_map/transpose(jvp())/dot_general | solution.py:21
  572.8 22.7 %convolution_convert_fusion.4 = bf16[1280,3072]{1,0:T(8,128)(2,1)} fusion(bf16[2048,3072]{1,0:T(8,128)(2,1)} %get-tuple-element.28, bf16[1,2048,1280]{1,2,0:T(8,128)(2,1)} %copy.10, f32[2048]{0:T(1024)S(1)} %copy-done.4), kind=kOutput, calls=%fused_computation.38 | convolution fusion | flops 16113991680 | bytes 25698304 | tf_op jit(solution)/shard_map/transpose(jvp())/dot_general | solution.py:21
  595.6 22.5 %fusion.42 = bf16[2048,1280]{0,1:T(8,128)(2,1)} fusion(bf16[2048,3072]{1,0:T(8,128)(2,1)} %get-tuple-element.28, bf16[1,1280,3072]{2,1,0:T(8,128)(2,1)} %all-gather.13.cloned.1.call-done), kind=kOutput, calls=%fused_computation.67 | convolution fusion | flops 16106127360 | bytes 25690112 | tf_op jit(solution)/shard_map/transpose(jvp())/dot_general | solution.py:21
  618.1 39.3 %reduce-scatter.13.cloned.1.call-done = bf16[160,3072]{1,0:T(8,128)(2,1)} async-done(((bf16[1280,3072]{1,0:T(8,128)(2,1)}), bf16[160,3072]{1,0:T(8,128)(2,1)}) %reduce-scatter.13.cloned.1.call-update) | async-done | bytes 983056 | tf_op jit(solution)/shard_map/reduce_scatter | solution.py:31
  657.4 66.4 %reduce-scatter.9.cloned.1.call-done = bf16[160,3072]{1,0:T(8,128)(2,1)} async-done(((bf16[1280,3072]{1,0:T(8,128)(2,1)}), bf16[160,3072]{1,0:T(8,128)(2,1)}) %reduce-scatter.9.cloned.1.call-update) | async-done | bytes 983056 | tf_op jit(solution)/shard_map/reduce_scatter | solution.py:31
  723.8 66.3 %reduce-scatter.7.cloned.1.call-done = bf16[160,3072]{1,0:T(8,128)(2,1)} async-done(((bf16[1280,3072]{1,0:T(8,128)(2,1)}), bf16[160,3072]{1,0:T(8,128)(2,1)}) %reduce-scatter.7.cloned.1.call-update) | async-done | bytes 983056 | tf_op jit(solution)/shard_map/reduce_scatter | solution.py:31
  790.1 29.6 %fusion.20 = (f32[2048]{0:T(1024)S(1)}, bf16[2048,1280]{0,1:T(8,128)(2,1)}) fusion(bf16[1,2048,1280]{1,2,0:T(8,128)(2,1)} %copy.10, bf16[2048,1280]{0,1:T(8,128)(2,1)} %fusion.42, bf16[1,1280,3072]{2,1,0:T(8,128)(2,1)} %all-gather.15.cloned.1.call-done, bf16[2048,3072]{1,0:T(8,128)(2,1)} %get-tuple-element.29, f32[2048,3072]{1,0:T(8,128)} %fusion.40), kind=kOutput, calls=%fused_computation.45 | convolution fusion | flops 16159602688 | bytes 61349888 | tf_op jit(solution)/shard_map/transpose(jvp())/dot_general | solution.py:22
  819.8 12.3 %fusion.67 = bf16[1,2048,1280]{1,2,0:T(8,128)(2,1)} fusion(bf16[2048,1280]{0,1:T(8,128)(2,1)} %fusion.68, bf16[2048,1280]{0,1:T(8,128)(2,1)} %get-tuple-element.31, bf16[1,2048,1280]{1,2,0:T(8,128)(2,1)} %copy.10, f32[2048]{0:T(1024)S(1)} %multiply_multiply_fusion, f32[2048]{0:T(1024)S(1)} %copy-done.4), kind=kLoop, calls=%fused_computation.76 | loop fusion | flops 18350080 | bytes 20987904 | tf_op jit(solution)/shard_map/broadcast_in_dim | solution.py:44
  832.1 7.9 copy.11
  839.9 94.1 %all-reduce.3.cloned.1.call-done = (bf16[1,160,3072]{2,1,0:T(8,128)(2,1)}, bf16[1,160,3072]{2,1,0:T(8,128)(2,1)}, bf16[1,160,3072]{2,1,0:T(8,128)(2,1)}, bf16[1,...) async-done(((bf16[1,160,3072]{2,1,0:T(8,128)(2,1)}, bf16[1,160,3072]{2,1,0:T(8,128)(2,1)}, bf16[1,160,3072]{2,1,0:T(8,128)(2,1)}, ...) | async-done | bytes 5898256 | tf_op jit(solution)/shard_map/psum | solution.py:31
  (64 shorter events, 21.8 us)
Async XLA Ops:
  7.2 6.1 copy-start
  7.2 54.0 %all-gather.13.cloned.1.call-start = ((), (), s32[]{:S(2)}) async-start(), calls=%async_computation.12 | async-start | bytes 8847360 | tf_op jit(solution)/shard_map/all_gather | solution.py:28
  10.3 100.8 %all-gather.15.cloned.1.call-start = ((), (), s32[]{:S(2)}) async-start(), calls=%async_computation.13 | async-start | bytes 8847360 | tf_op jit(solution)/shard_map/all_gather | solution.py:28
  13.3 147.6 %all-gather.17.cloned.1.call-start = ((), (), s32[]{:S(2)}) async-start(), calls=%async_computation.14 | async-start | bytes 8847360 | tf_op jit(solution)/shard_map/all_gather | solution.py:28
  14.7 195.8 %all-gather.21.cloned.1.call-start = ((), (), s32[]{:S(2)}) async-start(), calls=%async_computation.16 | async-start | bytes 8847360 | tf_op jit(solution)/shard_map/all_gather | solution.py:28
  15.3 245.5 %all-gather.23.cloned.1.call-start = ((), (), s32[]{:S(2)}) async-start(), calls=%async_computation.17 | async-start | bytes 8847360 | tf_op jit(solution)/shard_map/all_gather | solution.py:28
  15.9 295.2 %all-gather.19.cloned.1.call-start = ((), (), s32[]{:S(2)}) async-start(), calls=%async_computation.15 | async-start | bytes 8847360 | tf_op jit(solution)/shard_map/all_gather | solution.py:28
  16.5 601.6 %reduce-scatter.17.cloned.1.call-start = ((), (), s32[]{:S(2)}) async-start(), calls=%async_computation.11 | async-start | bytes 8847360 | tf_op jit(solution)/shard_map/reduce_scatter | solution.py:31
  28.0 0.6 copy-start.1
  28.6 82.5 %copy-start.3 = (f32[2048]{0:T(1024)}, f32[2048]{0:T(1024)S(1)}, u32[]{:S(2)}) copy-start(f32[2048]{0:T(1024)S(1)} %fusion.79) | copy-start | bytes 24580
  184.5 0.6 copy-start.8
  185.1 126.0 %copy-start.5 = (f32[2048]{0:T(1024)}, f32[2048]{0:T(1024)S(1)}, u32[]{:S(2)}) copy-start(f32[2048]{0:T(1024)S(1)} %fusion.80) | copy-start | bytes 24580
  378.5 21.9 %slice-start = ((s8[5242880]{0:T(1024)(128)(4,1)}), s8[1048576]{0:T(1024)(128)(4,1)S(1)}, s32[]{:S(2)}) async-start(s8[5242880]{0:T(1024)(128)(4,1)} %bitcast.92), calls=%async_computation.19 | async-start | bytes 2097152
  378.5 239.6 %reduce-scatter.15.cloned.1.call-start = ((), (), s32[]{:S(2)}) async-start(), calls=%async_computation.10 | async-start | bytes 8847360 | tf_op jit(solution)/shard_map/reduce_scatter | solution.py:31
  378.5 21.8 %slice-start.1 = ((s8[5242880]{0:T(1024)(128)(4,1)}), s8[4194304]{0:T(1024)(128)(4,1)S(1)}, s32[]{:S(2)}) async-start(s8[5242880]{0:T(1024)(128)(4,1)} %bitcast.92), calls=%async_computation.20 | async-start | bytes 8388608
  400.4 26.2 %copy-start.9 = (f32[2048]{0:T(1024)S(1)}, f32[2048]{0:T(1024)}, u32[]{:S(2)}) copy-start(f32[2048]{0:T(1024)} %copy-done.8) | copy-start | bytes 24580
  400.4 26.2 %copy-start.6 = (f32[2048]{0:T(1024)S(1)}, f32[2048]{0:T(1024)}, u32[]{:S(2)}) copy-start(f32[2048]{0:T(1024)} %copy-done.5) | copy-start | bytes 24580
  461.3 156.8 %reduce-scatter.11.cloned.1.call-start = ((), (), s32[]{:S(2)}) async-start(), calls=%async_computation.8 | async-start | bytes 8847360 | tf_op jit(solution)/shard_map/reduce_scatter | solution.py:31
  461.3 38.7 %copy-start.4 = (f32[2048]{0:T(1024)S(1)}, f32[2048]{0:T(1024)}, u32[]{:S(2)}) copy-start(f32[2048]{0:T(1024)} %copy-done.3) | copy-start | bytes 24580
  500.0 25.2 %copy-start.7 = (f32[2048]{0:T(1024)S(1)}, f32[2048]{0:T(1024)}, u32[]{:S(2)}) copy-start(f32[2048]{0:T(1024)} %copy-done.5) | copy-start | bytes 24580
  525.2 132.2 %reduce-scatter.13.cloned.1.call-start = ((), (), s32[]{:S(2)}) async-start(), calls=%async_computation.9 | async-start | bytes 8847360 | tf_op jit(solution)/shard_map/reduce_scatter | solution.py:31
  550.5 173.3 %reduce-scatter.9.cloned.1.call-start = ((), (), s32[]{:S(2)}) async-start(), calls=%async_computation.7 | async-start | bytes 8847360 | tf_op jit(solution)/shard_map/reduce_scatter | solution.py:31
  572.8 217.3 %reduce-scatter.7.cloned.1.call-start = ((), (), s32[]{:S(2)}) async-start(), calls=%async_computation.6 | async-start | bytes 8847360 | tf_op jit(solution)/shard_map/reduce_scatter | solution.py:31
  595.5 338.5 %all-reduce.3.cloned.1.call-start = ((), (), s32[]{:S(2)}) async-start(), calls=%async_computation.18 | async-start | bytes 11796480 | tf_op jit(solution)/shard_map/psum | solution.py:31
  790.1 29.6 %copy-start.2 = (f32[2048]{0:T(1024)S(1)}, f32[2048]{0:T(1024)}, u32[]{:S(2)}) copy-start(f32[2048]{0:T(1024)} %copy-done.1) | copy-start | bytes 24580
Sparse Core Ops, SparseCore 0:
  10.4 50.7 all-gather.12
  63.1 47.9 all-gather.14
  112.9 47.9 all-gather.16
  162.6 47.9 all-gather.20
  212.8 47.9 all-gather.22
  263.1 47.9 all-gather.18
  378.6 63.1 reduce-scatter.16
  461.4 63.1 reduce-scatter.14
  528.0 62.9 reduce-scatter.10
  594.3 62.9 reduce-scatter.12
  660.8 62.9 reduce-scatter.8
  727.1 62.9 reduce-scatter.6
  793.2 140.7 all-reduce.2
where the time goes:
time: 954 us; the launch traced here: 948 us
  matrix products  452 us (47%)
  waiting for transfers between devices  414 us (43%)
  other arithmetic  35.5 us (4%)
  local copies, waits for them, and re-layouts  32.2 us (3%)
  between operations  14.3 us (1%)
    reduce_scatter x6, waiting for transfers between devices, summed(): lax.psum_scatter(term, 's', scatter_dimension=0, tiled=True)  172 us
    dot_general x6, matrix products, layer(): up = jnp.dot(a, w['w_up'], preferred_element_type=jnp.float32)  164 us
    dot_general x6, matrix products, layer(): gate = jnp.dot(a, w['w_gate'], preferred_element_type=jnp.float32)  151 us
    all_gather x6, waiting for transfers between devices, fetched(): lax.all_gather(w[number], 's', axis=0, tiled=True)  146 us
    dot_general x5, matrix products, matmul(): jnp.dot(a, w, preferred_element_type=jnp.float32).astype(jnp.bfloat16)  136 us
    psum x1, waiting for transfers between devices, summed(): lax.psum(lax.psum_scatter(term, 's', scatter_dimension=0, tiled=True), 'r')  94.1 us
    unnamed x27, local copies, waits for them, and re-layouts  24.9 us
  transfers between devices with their start and end apart: 13, of which 10 were waited for; matrix products, arithmetic and copies ran while one was open for 46% of the time, Pallas kernels for 0%

commit v1 on v0

v1 whole, which is shorter than its diff:
```python
import functools

import jax
import jax.numpy as jnp
from jax import lax
from jax.experimental import pallas as pl
from jax.experimental.pallas import tpu as pltpu
from jax.sharding import PartitionSpec as P

MESH = pl.DeviceIdType.MESH
BF, F32 = jnp.bfloat16, jnp.float32
ANY = pl.BlockSpec(memory_space=pl.ANY)
VMEM_LIMIT = 66_000_000
TOK, D, FF = 2048, 1280, 3072


class Place:
    def __init__(self):
        self.z = lax.axis_index("r")
        self.s = lax.axis_index("s")
        self.x = self.s // 4
        self.y = (self.s // 2) % 2
        self.c = self.s % 2
        self.xs = self.s + 4 - 8 * self.x
        self.ys = self.s + 2 - 4 * self.y
        self.sib = self.s + 1 - 2 * self.c
        self.ds = self.xs + 2 - 4 * self.y
        self.to_x, self.to_y, self.to_sib = {"s": self.xs}, {"s": self.ys}, {"s": self.sib}
        self.to_z = {"r": 1 - self.z}

    def greet(self):
        barrier = pltpu.get_barrier_semaphore()
        for peer in (self.to_x, self.to_y, self.to_sib, self.to_z):
            pl.semaphore_signal(barrier, inc=1, device_id=peer, device_id_type=MESH)
        pl.semaphore_wait(barrier, 4)


def remote(src, dst, sems, k, peer):
    return pltpu.make_async_remote_copy(
        src_ref=src, dst_ref=dst, send_sem=sems[0].at[k], recv_sem=sems[1].at[k], device_id=peer, device_id_type=MESH
    )


class Gather:
    copies = 14
    stages = 4

    def __init__(self, own):
        self.inputs = [own]
        self.outputs = [jax.ShapeDtypeStruct((8, *own.shape), own.dtype)]
        self.scratch = [
            pltpu.VMEM(own.shape, own.dtype),
            pltpu.SemaphoreType.DMA((2,)),
            pltpu.SemaphoreType.DMA((self.copies,)),
            pltpu.SemaphoreType.DMA((self.copies,)),
        ]

    def stage(self, at, number, ins, outs, scratch):
        (own,), (full,), (held, local, *sems) = ins, outs, scratch
        rows = own.shape[0]
        low = 48 if rows == 160 else rows // 3
        both = rows - low
        plane = pl.ds(pl.multiple_of(at.z * low, 16), both)
        middle = pl.ds(low, both - low)
        mine = pl.ds(pl.multiple_of(at.z * both, 16), low)
        theirs = pl.ds(pl.multiple_of((1 - at.z) * both, 16), low)

        def copy(k):
            block = lambda s, r: full.at[s, r, :]
            return {
                0: lambda: remote(own.at[plane, :], block(at.s, plane), sems, 0, at.to_x),
                1: lambda: remote(own.at[plane, :], block(at.s, plane), sems, 1, at.to_y),
                2: lambda: remote(own, full.at[at.s], sems, 2, at.to_sib),
                3: lambda: remote(block(at.xs, middle), block(at.xs, middle), sems, 3, at.to_y),
                4: lambda: remote(block(at.ys, mine), block(at.ys, mine), sems, 4, at.to_x),
                5: lambda: remote(block(at.xs, mine), block(at.xs, mine), sems, 5, at.to_z),
                6: lambda: remote(block(at.ys, mine), block(at.ys, mine), sems, 6, at.to_z),
                7: lambda: remote(block(at.xs, plane), block(at.xs, plane), sems, 7, at.to_sib),
                8: lambda: remote(block(at.ys, plane), block(at.ys, plane), sems, 8, at.to_sib),
                9: lambda: remote(block(at.ds, mine), block(at.ds, mine), sems, 9, at.to_z),
                10: lambda: remote(block(at.ds, plane), block(at.ds, plane), sems, 10, at.to_sib),
                11: lambda: remote(block(at.xs, theirs), block(at.xs, theirs), sems, 11, at.to_sib),
                12: lambda: remote(block(at.ys, theirs), block(at.ys, theirs), sems, 12, at.to_sib),
                13: lambda: remote(block(at.ds, theirs), block(at.ds, theirs), sems, 13, at.to_sib),
            }[k]()

        into = lambda: pltpu.make_async_copy(own, held, local.at[0])
        out = lambda: pltpu.make_async_copy(held, full.at[at.s], local.at[1])
        wait, start = {
            0: ((), (0, 1, 2)),
            1: ((0, 1), (3, 4, 5, 6, 7, 8)),
            2: ((3, 4), (9, 10)),
            3: ((5, 6, 9), (11, 12, 13)),
            4: ((2, 7, 8, 10, 11, 12, 13), ()),
        }[number]
        if number == 1:
            into().wait()
            out().start()
        for k in wait:
            copy(k).wait_recv()
        for k in start:
            copy(k).start()
        if number == 0:
            into().start()
        if number == 4:
            for k in range(self.copies):
                copy(k).wait_send()
            out().wait()


class Spread:
    stages = 0

    def __init__(self, part):
        _, _, rows, columns = part.shape
        self.inputs = [part]
        self.outputs = [jax.ShapeDtypeStruct((2, rows // 2, columns), BF)] * 2
        self.scratch = [pltpu.SemaphoreType.DMA((2,)), pltpu.SemaphoreType.DMA((2,))]

    def pairs(self, at, ins, outs):
        (part,), (first, second) = ins, outs
        half = part.shape[2] // 2
        return [
            (part.at[1 - at.x, :, pl.ds(0, half), :], first, at.to_x),
            (part.at[:, 1 - at.y, pl.ds(half, half), :], second, at.to_y),
        ]

    def stage(self, at, number, ins, outs, scratch):
        for k, (src, dst, peer) in enumerate(self.pairs(at, ins, outs)):
            copy = remote(src, dst, scratch, k, peer)
            if number == 0:
                copy.start()
            else:
                copy.wait()


class Cross(Spread):
    def __init__(self, part):
        self.inputs = [part]
        self.outputs = [jax.ShapeDtypeStruct(part.shape, BF)]
        self.scratch = [pltpu.SemaphoreType.DMA((2,)), pltpu.SemaphoreType.DMA((2,))]

    def pairs(self, at, ins, outs):
        (part,), (got,) = ins, outs
        return [(part.at[0], got.at[0], at.to_y), (part.at[1], got.at[1], at.to_x)]


class Rise(Cross):
    def pairs(self, at, ins, outs):
        (part,), (got,) = ins, outs
        return [(part, got, at.to_z)]


def call(name, body, grid, ins, in_specs, outs, out_specs, scratch, comms, number, flops, points=None):
    n_in, n_out, n_scratch = len(ins), len(outs), len(scratch)
    steps = functools.reduce(lambda a, b: a * b, grid, 1)
    points = points or {}

    def kernel(*refs):
        refs = list(refs)
        take = lambda n: [refs.pop(0) for _ in range(n)]
        i_refs = take(n_in)
        ci = [take(len(m.inputs)) for m in comms]
        o_refs = take(n_out)
        co = [take(len(m.outputs)) for m in comms]
        s_refs = take(n_scratch)
        cs = [take(len(m.scratch)) for m in comms]
        at = Place()
        step = pl.program_id(0)
        if len(grid) == 2:
            step = step * grid[1] + pl.program_id(1)

        @pl.when(step == 0)
        def _():
            at.greet()
            for m, i, o, s in zip(comms, ci, co, cs):
                m.stage(at, 0, i, o, s)

        last = {}
        for index, m in enumerate(comms):
            for stage in range(1, m.stages):
                last.setdefault(min(points.get((index, stage), steps - 1), steps - 1), []).append((index, stage))
        for when, events in last.items():
            if when < steps - 1:

                @pl.when(step == when)
                def _(events=events):
                    for index, stage in events:
                        comms[index].stage(at, stage, ci[index], co[index], cs[index])

        body(at, step, i_refs, o_refs, s_refs)

        @pl.when(step == steps - 1)
        def _():
            late = last.get(steps - 1, [])
            for stage in range(1, Gather.stages):
                for index, wanted in late:
                    if wanted == stage:
                        comms[index].stage(at, stage, ci[index], co[index], cs[index])
            for m, i, o, s in zip(comms, ci, co, cs):
                m.stage(at, max(m.stages, 1), i, o, s)

    flat = lambda key: [v for m in comms for v in getattr(m, key)]
    moved = flat("inputs")
    results = pl.pallas_call(
        kernel,
        grid=grid,
        in_specs=list(in_specs) + [ANY] * len(moved),
        out_specs=list(out_specs) + [ANY] * len(flat("outputs")),
        out_shape=list(outs) + flat("outputs"),
        scratch_shapes=list(scratch) + flat("scratch"),
        compiler_params=pltpu.CompilerParams(
            collective_id=number,
            has_side_effects=True,
            vmem_limit_bytes=VMEM_LIMIT,
            dimension_semantics=("arbitrary",) * len(grid),
        ),
        cost_estimate=pl.CostEstimate(flops=flops, bytes_accessed=1 << 24, transcendentals=0),
        name=name,
    )(*ins, *moved)
    results = list(results)
    mine, results = results[:n_out], results[n_out:]
    got = []
    for m in comms:
        got.append(results[: len(m.outputs)])
        results = results[len(m.outputs) :]
    return mine, got


def scale_of(wide):
    return lax.rsqrt(jnp.mean(wide * wide, -1, keepdims=True) + 1e-6)


def shape(dims, dtype=BF):
    return jax.ShapeDtypeStruct(dims, dtype)


def once(dims, index):
    return pl.BlockSpec(dims, index, pipeline_mode=pl.Buffered(1))


def dot(a, b, ca=1, cb=0):
    return lax.dot_general(a, b, (((ca,), (cb,)), ((), ())), preferred_element_type=F32)


def first_norm(h, comms, number):
    def body(at, step, ins, outs, scratch):
        wide = ins[0][...].astype(F32)
        outs[0][...] = (wide * scale_of(wide)).astype(BF)

    tile = pl.BlockSpec((512, D), lambda i: (i, 0))
    (a,), got = call("fetch", body, (4,), [h], [tile], [shape((TOK, D))], [tile], [], comms, number, 10**7)
    return a, got


def gate_up(a, wg, wu, comms, number, points):
    rows, cols = 1024, 512

    def body(at, step, ins, outs, scratch):
        a_ref, g_ref, u_ref = ins
        act, gate, up = outs
        start = pl.program_id(1) * rows
        g_w = g_ref[...].reshape(D, cols)
        u_w = u_ref[...].reshape(D, cols)
        for k in range(rows // 512):
            part = pl.ds(k * 512, 512)
            left = a_ref[pl.ds(pl.multiple_of(start + k * 512, 512), 512), :]
            g = dot(left, g_w)
            u = dot(left, u_w)
            gate[part, :] = g
            up[part, :] = u
            act[part, :] = (g * jax.nn.sigmoid(g) * u).astype(BF)

    weight = pl.BlockSpec((8, 160, cols), lambda j, i: (0, 0, j))
    tile = pl.BlockSpec((rows, cols), lambda j, i: (i, j))
    return call(
        "gate_up", body, (FF // cols, TOK // rows), [a, wg, wu], [once((TOK, D), lambda j, i: (0, 0)), weight, weight],
        [shape((TOK, FF)), shape((TOK, FF), F32), shape((TOK, FF), F32)], [tile] * 3, [], comms, number, 4 * TOK * D * FF, points,
    )


def down(act, wd, h, comms, number, points):
    rows = 256

    def body(at, step, ins, outs, scratch):
        act_ref, w_ref, h_ref = ins
        out = dot(act_ref[...], w_ref[...].reshape(FF, D)).astype(BF)
        new = (h_ref[...].astype(F32) + out.astype(F32)).astype(BF)
        outs[0][...] = new
        wide = new.astype(F32)
        outs[1][...] = (wide * scale_of(wide)).astype(BF)

    tile = pl.BlockSpec((rows, D), lambda i: (i, 0))
    return call(
        "down", body, (TOK // rows,), [act, wd, h], [pl.BlockSpec((rows, FF), lambda i: (i, 0)), once((8, 384, D), lambda i: (0, 0, 0)), tile],
        [shape((TOK, D)), shape((TOK, D))], [tile, tile], [], comms, number, 2 * TOK * D * FF, points,
    )


def by_act(dy, wd, gate, up, comms, number):
    rows, cols = 512, 768

    def body(at, step, ins, outs, scratch):
        dy_ref, w_ref, g_ref, u_ref = ins
        left = dy_ref[pl.ds(pl.multiple_of(pl.program_id(1) * rows, rows), rows), :]
        da = dot(left, w_ref[...].reshape(cols, D), 1, 1).astype(BF).astype(F32)
        g, u = g_ref[...], u_ref[...]
        sig = jax.nn.sigmoid(g)
        silu = g * sig
        outs[0][0] = (da * u * (sig + silu * (1 - sig))).astype(BF)
        outs[0][1] = (da * silu).astype(BF)

    tile = pl.BlockSpec((rows, cols), lambda j, i: (i, j))
    return call(
        "by_act", body, (FF // cols, TOK // rows), [dy, wd, gate, up],
        [once((TOK, D), lambda j, i: (0, 0)), pl.BlockSpec((2, 384, D), lambda j, i: (j, 0, 0)), tile, tile],
        [shape((2, TOK, FF))], [pl.BlockSpec((2, rows, cols), lambda j, i: (0, i, j))], [], comms, number, 2 * TOK * D * FF,
    )


def by_state(dgu, wg, wu, h, dy, comms, number):
    rows = 256

    def body(at, step, ins, outs, scratch):
        d_ref, g_ref, u_ref, h_ref, dy_ref = ins
        first = dot(d_ref[0], g_ref[...].reshape(D, FF), 1, 1).astype(BF)
        second = dot(d_ref[1], u_ref[...].reshape(D, FF), 1, 1).astype(BF)
        da = (first.astype(F32) + second.astype(F32)).astype(BF).astype(F32)
        wide = h_ref[...].astype(F32)
        scale = scale_of(wide)
        along = jnp.sum(da * wide, -1, keepdims=True)
        dh = da * scale - wide * (along * scale * scale * scale * (1.0 / D))
        outs[0][...] = (dy_ref[...].astype(F32) + dh.astype(BF).astype(F32)).astype(BF)

    tile = pl.BlockSpec((rows, D), lambda i: (i, 0))
    weight = once((8, 160, FF), lambda i: (0, 0, 0))
    return call(
        "by_state", body, (TOK // rows,), [dgu, wg, wu, h, dy],
        [pl.BlockSpec((2, rows, FF), lambda i: (0, i, 0)), weight, weight, tile, tile],
        [shape((TOK, D))], [tile], [], comms, number, 4 * TOK * D * FF,
    )


def by_down(act, dy, comms, number):
    n = 4

    def body(at, step, ins, outs, scratch):
        act_ref, dy_ref = ins
        term, mine, send, recv, *sems = scratch

        def copy(t, slot):
            return remote(send.at[slot], recv.at[t], sems, t, at.to_sib)

        @pl.when(step > 0)
        def _():
            copy(step - 1, (step - 1) % 2).wait_recv()
            total = mine[...].astype(F32) + recv[step - 1].astype(F32)
            outs[0][0] = total.astype(BF)
            outs[1][0] = total

        @pl.when(step < n)
        def _():
            @pl.when(step > 1)
            def _():
                copy(step - 2, step % 2).wait_send()

            for k in range(2):
                term[k] = dot(act_ref[:, k * 384 : (k + 1) * 384], dy_ref[...], 0, 0).astype(BF)
            send[step % 2] = term[1 - at.c]
            mine[...] = term[at.c]
            copy(step, step % 2).start()

        @pl.when(step == n)
        def _():
            copy(n - 2, n % 2).wait_send()
            copy(n - 1, (n - 1) % 2).wait_send()

    before = lambda i: (jnp.maximum(i - 1, 0), 0, 0)
    out = pl.BlockSpec((1, 384, D), before)
    return call(
        "by_down", body, (n + 1,), [act, dy],
        [pl.BlockSpec((TOK, 768), lambda i: (0, jnp.minimum(i, n - 1))), once((TOK, D), lambda i: (0, 0))],
        [shape((n, 384, D)), shape((n, 384, D), F32)], [out, out],
        [pltpu.VMEM((2, 384, D), BF), pltpu.VMEM((384, D), BF), pltpu.VMEM((2, 384, D), BF), pltpu.VMEM((n, 384, D), BF),
         pltpu.SemaphoreType.DMA((n,)), pltpu.SemaphoreType.DMA((n,))],
        comms, number, 2 * TOK * D * FF,
    )


def by_gate_up(a, dgu, comms, number):
    cols = 512
    each = FF // cols
    n = 2 * each

    def body(at, step, ins, outs, scratch):
        a_ref, d_ref = ins
        across, term, mine, send, recv, *sems = scratch

        def copy(t, slot):
            return remote(send.at[slot], recv.at[t], sems, t, at.to_sib)

        @pl.when(step == 0)
        def _():
            for k in range(TOK // 256):
                across[:, k * 256 : (k + 1) * 256] = a_ref[k * 256 : (k + 1) * 256, :].T

        @pl.when(step > 0)
        def _():
            copy(step - 1, (step - 1) % 2).wait_recv()
            total = mine[...].astype(F32) + recv[step - 1].astype(F32)
            outs[0][:, 0] = total.astype(BF)
            outs[1][:, 0] = total

        @pl.when(step < n)
        def _():
            @pl.when(step > 1)
            def _():
                copy(step - 2, step % 2).wait_send()

            term[...] = dot(across[...], d_ref[0]).astype(BF).reshape(8, 160, cols)
            for k in range(4):
                send[step % 2, k] = term[2 * k + 1 - at.c]
                mine[k] = term[2 * k + at.c]
            copy(step, step % 2).start()

        @pl.when(step == n)
        def _():
            copy(n - 2, n % 2).wait_send()
            copy(n - 1, (n - 1) % 2).wait_send()

    def before(i):
        t = jnp.maximum(i - 1, 0)
        return 0, t // each, 0, t % each

    def now(i):
        t = jnp.minimum(i, n - 1)
        return t // each, 0, t % each

    out = pl.BlockSpec((4, 1, 160, cols), before)
    return call(
        "by_gate_up", body, (n + 1,), [a, dgu], [once((TOK, D), lambda i: (0, 0)), pl.BlockSpec((1, TOK, cols), now)],
        [shape((4, 2, 160, FF)), shape((4, 2, 160, FF), F32)], [out, out],
        [pltpu.VMEM((D, TOK), BF), pltpu.VMEM((8, 160, cols), BF), pltpu.VMEM((4, 160, cols), BF), pltpu.VMEM((2, 4, 160, cols), BF),
         pltpu.VMEM((n, 4, 160, cols), BF), pltpu.SemaphoreType.DMA((n,)), pltpu.SemaphoreType.DMA((n,))],
        comms, number, 4 * TOK * D * FF,
    )


def only(comms, number):
    def body(at, step, ins, outs, scratch):
        outs[0][...] = jnp.zeros((8, 128), F32)

    tile = pl.BlockSpec((8, 128), lambda i: (0, 0))
    return call("exchange", body, (1,), [], [], [shape((8, 128), F32)], [tile], [], comms, number, 10**6)[1]


class Sum:
    def __init__(self, at, part, wide, rows, columns):
        self.at, self.rows = at, rows
        self.part, self.wide = part.reshape(2, 2, rows, columns), wide.reshape(2, 2, rows, columns)

    def pick(self, x, y, second):
        half = self.rows // 2
        block = lax.dynamic_slice(self.wide, (x, y, half * second, 0), (1, 1, half, self.wide.shape[3]))
        return block[0, 0]

    def spread(self):
        return Spread(self.part)

    def cross(self, got):
        self.a, self.b = got
        at = self.at
        low = self.pick(at.x, 1 - at.y, 0) + lax.dynamic_index_in_dim(self.a, 1 - at.y, 0, False).astype(F32)
        high = self.pick(1 - at.x, at.y, 1) + lax.dynamic_index_in_dim(self.b, 1 - at.x, 0, False).astype(F32)
        return Cross(jnp.stack([low, high]).astype(BF))

    def rise(self, got):
        (c,) = got
        at = self.at
        low = self.pick(at.x, at.y, 0) + lax.dynamic_index_in_dim(self.a, at.y, 0, False).astype(F32) + c[0].astype(F32)
        high = self.pick(at.x, at.y, 1) + lax.dynamic_index_in_dim(self.b, at.x, 0, False).astype(F32) + c[1].astype(F32)
        self.total = jnp.stack([low, high])
        return self.total.astype(BF)

    def end(self, got):
        return (self.total + got.astype(F32)).astype(BF)


def solution(mesh):
    def step(x, dy, w_gate, w_up, w_down):
        x, dy = x[0], dy[0]
        at = Place()
        g, u, d = ([w[0], w[1]] for w in (w_gate, w_up, w_down))
        a0, ((g0,), (u0,)) = first_norm(x, [Gather(g[0]), Gather(u[0])], 0)
        points = {(0, 1): 5, (0, 2): 9, (1, 1): 9}
        (act0, gate0, up0), ((d0,), (g1,)) = gate_up(a0, g0, u0, [Gather(d[0]), Gather(g[1])], 1, points)
        (h1, a1), ((u1,),) = down(act0, d0, x, [Gather(u[1])], 2, {(0, 1): 6})
        (act1, gate1, up1), ((d1,),) = gate_up(a1, g1, u1, [Gather(d[1])], 3, {(0, 1): 5, (0, 2): 8, (0, 3): 10})

        def sums(pair, rows, columns):
            return Sum(at, *pair, rows, columns)

        pair, _ = by_down(act1, dy, [], 4)
        s_d1 = sums(pair, 384, D)
        (dgu1,), (got,) = by_act(dy, d1, gate1, up1, [s_d1.spread()], 5)
        pair, (got,) = by_gate_up(a1, dgu1, [s_d1.cross(got)], 6)
        s_gu1 = sums(pair, 320, FF)
        (dh1,), (got, (z_d1,)) = by_state(dgu1, g1, u1, h1, dy, [s_gu1.spread(), Rise(s_d1.rise(got))], 7)
        pair, (got,) = by_down(act0, dh1, [s_gu1.cross(got)], 8)
        s_d0 = sums(pair, 384, D)
        up_gu1 = s_gu1.rise(got)
        (dgu0,), (got, (z_g1,)) = by_act(dh1, d0, gate0, up0, [s_d0.spread(), Rise(up_gu1[0])], 9)
        pair, (got, (z_u1,)) = by_gate_up(a0, dgu0, [s_d0.cross(got), Rise(up_gu1[1])], 10)
        s_gu0 = sums(pair, 320, FF)
        (dx,), (got, (z_d0,)) = by_state(dgu0, g0, u0, x, dh1, [s_gu0.spread(), Rise(s_d0.rise(got))], 11)
        (got,) = only([s_gu0.cross(got)], 12)
        up_gu0 = s_gu0.rise(got)
        ((z_gu0,),) = only([Rise(up_gu0)], 13)

        gu1 = s_gu1.end(jnp.stack([z_g1, z_u1]))
        gu0 = s_gu0.end(z_gu0)
        down1, down0 = s_d1.end(z_d1).reshape(384, D), s_d0.end(z_d0).reshape(384, D)
        return dx[None], jnp.stack([gu0[0], gu1[0]]), jnp.stack([gu0[1], gu1[1]]), jnp.stack([down0, down1])

    states, cut = P(("rep", "r", "s"), None, None), P(None, "s", None)
    return jax.shard_map(
        step,
        mesh=mesh,
        in_specs=(states, states) + (cut,) * 3,
        out_specs=(states,) + (P("rep", "s", None),) * 3,
        check_vma=False,
    )
```

time: 954 us -> 775 us (0.81)
  Pallas kernels: 0 us -> 701 us
  matrix products: 452 us -> 0 us
  waiting for transfers between devices: 414 us -> 0 us
  between operations: 14.3 us -> 1.51 us
  local copies, waits for them, and re-layouts: 32.2 us -> 21.1 us
    pallas_call x0 -> x14, Pallas kernels: none -> 701 us  [call(): pl.pallas_call(kernel, grid=grid, in_specs=list(in_specs) + [ANY] * len(m...]
    dot_general x17 -> x0, matrix products: 452 us -> none  [the longest x6 164 us: layer(): up = jnp.dot(a, w['w_up'], preferred_element_type=jnp.float32)]
    reduce_scatter x6 -> x0, waiting for transfers between devices: 172 us -> none  [summed(): lax.psum_scatter(term, 's', scatter_dimension=0, tiled=True)]
    all_gather x6 -> x0, waiting for transfers between devices: 146 us -> none  [fetched(): lax.all_gather(w[number], 's', axis=0, tiled=True)]
    psum x1 -> x0, waiting for transfers between devices: 94.1 us -> none  [summed(): lax.psum(lax.psum_scatter(term, 's', scatter_dimension=0, tiled=True), 'r')]
    add x0 -> x4, other arithmetic: none -> 12.7 us  [rise(): self.pick(at.x, at.y, 0)]
    unnamed x27 -> x39, local copies, waits for them, and re-layouts: 24.9 us -> 12.5 us
    broadcast_in_dim x1 -> x0, other arithmetic: 12.3 us -> none  [step(): by_h[None]]
  transfers between devices with their start and end apart: 13 -> 0, of which waited for: 10 -> 0; matrix products, arithmetic and copies ran while one was open for 46% -> 0% of each run, Pallas kernels for 0% -> 0%
where the time goes in v1:
time: 775 us; the launch traced here: 765 us
  Pallas kernels  701 us (90%)
  other arithmetic  42.1 us (5%)
  local copies, waits for them, and re-layouts  21.1 us (3%)
    pallas_call x14, Pallas kernels, call(): pl.pallas_call(kernel, grid=grid, in_specs=list(in_specs) + [ANY] * len(m...  701 us

profile of v1, /device:TPU:0, one launch (start us, length us, event | category | flops | bytes accessed | tf_op | source)
XLA Modules:
  0.0 765.3 jit_solution(2070389672943913683)
XLA Ops:
  0.6 4.1 slice_bitcast_fusion.3
  4.7 66.4 %fetch.1 = (bf16[2048,1280]{1,0:T(8,128)(2,1)}, bf16[8,160,3072]{2,1,0:T(8,128)(2,1)}, bf16[8,160,3072]{2,1,0:T(8,128)(2,1)}) custom-call(bf16[2048,1280]{1,0:T(8,128)(2,1)} %bitcast.98, bf16[160,3072]{1,0:T(8,128)(2,1)} %get-tuple-element.120.refs_1_, bf16[160,3072]{1,0:T(8,128)(2,1)} %get-tuple-element.117.refs_2_), custom_call_target="tpu_custom_call" | custom-call | flops 10000000 | bytes 16777216 | tf_op jit(solution)/shard_map/fetch/pallas_call | solution.py:205
  71.2 2.9 slice_bitcast_fusion.2
  74.1 75.0 %gate_up.2 = (bf16[2048,3072]{1,0:T(8,128)(2,1)}, f32[2048,3072]{1,0:T(8,128)}, f32[2048,3072]{1,0:T(8,128)}, bf16[8,384,1280]{2,1,0:T(8,128)(2,1)}, bf16[8,160,3072]{2,1,0:T(8,128)(2,1)}) custom-call(bf16[2048,1280]{1,0:T(8,128)(2,1)} %get-tuple-element.48.refs_0_, bf16[8,160,3072]{2,1,0:T(8,128)(2,1)} %get-tuple-element.49.refs_1_, ...), custom_call_target="tpu_custom_call" | custom-call | flops 32212254720 | bytes 16777216 | tf_op jit(solution)/shard_map/gate_up/pallas_call | solution.py:205
  149.0 45.2 %down.1 = (bf16[2048,1280]{1,0:T(8,128)(2,1)}, bf16[2048,1280]{1,0:T(8,128)(2,1)}, bf16[8,160,3072]{2,1,0:T(8,128)(2,1)}) custom-call(bf16[2048,3072]{1,0:T(8,128)(2,1)} %get-tuple-element.51.refs_0_, bf16[8,384,1280]{2,1,0:T(8,128)(2,1)} %get-tuple-element.52.refs_1_, bf16[2048,1280]{1,0:T(8,128)(2,1)} %bitcast.99, bf16[160,3072]{1,0:T(8,128)(2,1)} %get-tuple-element.116.refs_3_), custom_call_target="tpu_custom_call" | custom-call | flops 16106127360 | bytes 16777216 | tf_op jit(solution)/shard_map/down/pallas_call | solution.py:205
  194.2 52.1 %gate_up.3 = (bf16[2048,3072]{1,0:T(8,128)(2,1)}, f32[2048,3072]{1,0:T(8,128)}, f32[2048,3072]{1,0:T(8,128)}, bf16[8,384,1280]{2,1,0:T(8,128)(2,1)}) custom-call(bf16[2048,1280]{1,0:T(8,128)(2,1)} %get-tuple-element.53.refs_0_, bf16[8,160,3072]{2,1,0:T(8,128)(2,1)} %get-tuple-element.54.refs_1_, bf16[8,160,3072]{2,1,0:T(8,128)(2,1)} %get-tuple-element.55.refs_2_, ...), custom_call_target="tpu_custom_call" | custom-call | flops 32212254720 | bytes 16777216 | tf_op jit(solution)/shard_map/gate_up/pallas_call | solution.py:205
  246.3 34.8 %by_down.2 = (bf16[4,384,1280]{2,1,0:T(8,128)(2,1)}, f32[4,384,1280]{2,1,0:T(8,128)}) custom-call(bf16[2048,3072]{1,0:T(8,128)(2,1)} %get-tuple-element.59.refs_0_, bf16[2048,1280]{1,0:T(8,128)(2,1)} %bitcast.95), custom_call_target="tpu_custom_call" | custom-call | flops 16106127360 | bytes 16777216 | tf_op jit(solution)/shard_map/by_down/pallas_call | solution.py:205
  281.1 41.2 %by_act.2 = (bf16[2,2048,3072]{2,1,0:T(8,128)(2,1)}, bf16[2,192,1280]{2,1,0:T(8,128)(2,1)}, bf16[2,192,1280]{2,1,0:T(8,128)(2,1)}) custom-call(bf16[2048,1280]{1,0:T(8,128)(2,1)} %bitcast.96, bf16[8,384,1280]{2,1,0:T(8,128)(2,1)} %get-tuple-element.56.refs_1_, f32[2048,3072]{1,0:T(8,128)} %get-tuple-element.57.refs_2_, ...), custom_call_target="tpu_custom_call" | custom-call | flops 16106127360 | bytes 16777216 | tf_op jit(solution)/shard_map/by_act/pallas_call | solution.py:205
  322.4 2.0 fusion.19
  325.4 68.0 %by_gate_up.2 = (bf16[4,2,160,3072]{3,2,1,0:T(8,128)(2,1)}, f32[4,2,160,3072]{3,2,1,0:T(8,128)}, bf16[2,192,1280]{2,1,0:T(8,128)(2,1)}) custom-call(bf16[2048,1280]{1,0:T(8,128)(2,1)} %get-tuple-element.53.refs_0_, bf16[2,2048,3072]{2,1,0:T(8,128)(2,1)} %get-tuple-element.61.refs_1_.refs_0_, bf16[2,192,1280]{2,1,0:T(8,128)(2,1)} %pad_maximum_fusion.9.refs_2_), custom_call_target="tpu_custom_call" | custom-call | flops 32212254720 | bytes 16777216 | tf_op jit(solution)/shard_map/by_gate_up/pallas_call | solution.py:205
  393.4 2.2 fusion.17
  397.7 52.5 %by_state.2 = (bf16[2048,1280]{1,0:T(8,128)(2,1)}, bf16[2,160,3072]{2,1,0:T(8,128)(2,1)}, bf16[2,160,3072]{2,1,0:T(8,128)(2,1)}, bf16[2,192,1280]{2,1,0:T(8,128)(2,1)}) custom-call(bf16[2,2048,3072]{2,1,0:T(8,128)(2,1)} %get-tuple-element.61.refs_1_.refs_0_, bf16[8,160,3072]{2,1,0:T(8,128)(2,1)} %get-tuple-element.54.refs_1_, ...), custom_call_target="tpu_custom_call" | custom-call | flops 32212254720 | bytes 16777216 | tf_op jit(solution)/shard_map/by_state/pallas_call | solution.py:205
  450.2 3.3 fusion.9
  453.4 1.4 pad_maximum_fusion.3.refs_2_
  454.9 34.5 %by_down.3 = (bf16[4,384,1280]{2,1,0:T(8,128)(2,1)}, f32[4,384,1280]{2,1,0:T(8,128)}, bf16[2,160,3072]{2,1,0:T(8,128)(2,1)}) custom-call(bf16[2048,3072]{1,0:T(8,128)(2,1)} %get-tuple-element.51.refs_0_, bf16[2048,1280]{1,0:T(8,128)(2,1)} %get-tuple-element.68.refs_1_.refs_0_.refs_4_, bf16[2,160,3072]{2,1,0:T(8,128)(2,1)} %pad_maximum_fusion.3.refs_2_), custom_call_target="tpu_custom_call" | custom-call | flops 16106127360 | bytes 16777216 | tf_op jit(solution)/shard_map/by_down/pallas_call | solution.py:205
  489.4 4.1 fusion.7
  496.8 41.8 %by_act.3 = (bf16[2,2048,3072]{2,1,0:T(8,128)(2,1)}, bf16[2,192,1280]{2,1,0:T(8,128)(2,1)}, bf16[2,192,1280]{2,1,0:T(8,128)(2,1)}, bf16[160,3072]{1,0:T(8,128)(2,1)}) custom-call(bf16[2048,1280]{1,0:T(8,128)(2,1)} %get-tuple-element.68.refs_1_.refs_0_.refs_4_, bf16[8,384,1280]{2,1,0:T(8,128)(2,1)} %get-tuple-element.52.refs_1_, ...), custom_call_target="tpu_custom_call" | custom-call | flops 16106127360 | bytes 16777216 | tf_op jit(solution)/shard_map/by_act/pallas_call | solution.py:205
  538.5 2.0 fusion.15
  541.5 67.3 %by_gate_up.3 = (bf16[4,2,160,3072]{3,2,1,0:T(8,128)(2,1)}, f32[4,2,160,3072]{3,2,1,0:T(8,128)}, bf16[2,192,1280]{2,1,0:T(8,128)(2,1)}, bf16[160,3072]{1,0:T(8,128)(2,1)}) custom-call(bf16[2048,1280]{1,0:T(8,128)(2,1)} %get-tuple-element.48.refs_0_, bf16[2,2048,3072]{2,1,0:T(8,128)(2,1)} %get-tuple-element.76.refs_1_.refs_0_, ...), custom_call_target="tpu_custom_call" | custom-call | flops 32212254720 | bytes 16777216 | tf_op jit(solution)/shard_map/by_gate_up/pallas_call | solution.py:205
  608.9 2.3 fusion.13
  613.2 52.7 %by_state.3 = (bf16[2048,1280]{1,0:T(8,128)(2,1)}, bf16[2,160,3072]{2,1,0:T(8,128)(2,1)}, bf16[2,160,3072]{2,1,0:T(8,128)(2,1)}, bf16[2,192,1280]{2,1,0:T(8,128)(2,1)}) custom-call(bf16[2,2048,3072]{2,1,0:T(8,128)(2,1)} %get-tuple-element.76.refs_1_.refs_0_, bf16[8,160,3072]{2,1,0:T(8,128)(2,1)} %get-tuple-element.49.refs_1_, ...), custom_call_target="tpu_custom_call" | custom-call | flops 32212254720 | bytes 16777216 | tf_op jit(solution)/shard_map/by_state/pallas_call | solution.py:205
  666.0 1.9 add_convert_fusion.3
  668.6 1.4 pad_maximum_fusion.8
  671.4 2.7 fusion.4
  674.1 1.4 pad_maximum_fusion.5.refs_0_
  675.6 24.3 %exchange.2 = (f32[8,128]{1,0:T(8,128)}, bf16[2,160,3072]{2,1,0:T(8,128)(2,1)}) custom-call(bf16[2,160,3072]{2,1,0:T(8,128)(2,1)} %pad_maximum_fusion.5.refs_0_), custom_call_target="tpu_custom_call" | custom-call | flops 1000000 | bytes 16777216 | tf_op jit(solution)/shard_map/exchange/pallas_call | solution.py:205
  699.8 4.1 fusion.5
  705.8 1.6 fusion.refs_0_
  707.4 44.9 %exchange.3 = (f32[8,128]{1,0:T(8,128)}, bf16[2,160,3072]{2,1,0:T(8,128)(2,1)}) custom-call(bf16[2,160,3072]{2,1,0:T(8,128)(2,1)} %fusion.refs_0_), custom_call_target="tpu_custom_call" | custom-call | flops 1000000 | bytes 16777216 | tf_op jit(solution)/shard_map/exchange/pallas_call | solution.py:205
  752.4 3.4 add_convert_fusion.1
  758.8 1.4 pad_maximum_fusion.7
  762.5 2.4 copy.10
  (50 shorter events, 18.6 us)
Async XLA Ops:
  325.4 68.0 %copy-start.13 = (bf16[2,192,1280]{2,1,0:T(8,128)(2,1)S(1)}, bf16[2,192,1280]{2,1,0:T(8,128)(2,1)}, u32[]{:S(2)}) copy-start(bf16[2,192,1280]{2,1,0:T(8,128)(2,1)} %get-tuple-element.64) | copy-start | bytes 2949124
  395.7 1.0 copy-start.6
  395.7 2.0 copy-start.8
  493.4 1.3 copy-start
  493.5 1.9 copy-start.2
  611.2 0.9 copy-start.10
  666.0 1.9 copy-start.7
  666.0 2.1 copy-start.9
  666.0 2.4 copy-start.16
  668.6 2.3 copy-start.11
  668.6 2.8 copy-start.12
  703.9 1.3 copy-start.4
  703.9 1.9 copy-start.5
  752.4 3.6 copy-start.14
  752.4 3.6 copy-start.15
  755.8 1.5 copy-start.1
  755.9 2.1 copy-start.3
  758.6 3.3 slice-start
  758.8 3.8 slice-start.1

commit v2 on v0

v2 whole, which is shorter than its diff:
```python
import functools

import jax
import jax.numpy as jnp
from jax import lax
from jax.experimental import pallas as pl
from jax.experimental.pallas import tpu as pltpu
from jax.sharding import PartitionSpec as P

MESH = pl.DeviceIdType.MESH
END = (1 << 30, 99)
BF, F32 = jnp.bfloat16, jnp.float32
ANY = pl.BlockSpec(memory_space=pl.ANY)
VMEM_LIMIT = 66_000_000
TOK, D, FF = 2048, 1280, 3072


class Place:
    def __init__(self):
        self.z = lax.axis_index("r")
        self.s = lax.axis_index("s")
        self.x = self.s // 4
        self.y = (self.s // 2) % 2
        self.c = self.s % 2
        self.xs = self.s + 4 - 8 * self.x
        self.ys = self.s + 2 - 4 * self.y
        self.sib = self.s + 1 - 2 * self.c
        self.ds = self.xs + 2 - 4 * self.y
        self.to_x, self.to_y, self.to_sib = {"s": self.xs}, {"s": self.ys}, {"s": self.sib}
        self.to_z = {"r": 1 - self.z}

    def greet(self):
        barrier = pltpu.get_barrier_semaphore()
        for peer in (self.to_x, self.to_y, self.to_sib, self.to_z):
            pl.semaphore_signal(barrier, inc=1, device_id=peer, device_id_type=MESH)
        pl.semaphore_wait(barrier, 4)


def remote(src, dst, sems, k, peer):
    return pltpu.make_async_remote_copy(
        src_ref=src, dst_ref=dst, send_sem=sems[0].at[k], recv_sem=sems[1].at[k], device_id=peer, device_id_type=MESH
    )


class Gather:
    copies = 14
    last = 4

    def __init__(self, whole, layer, blocks=1, only=None, onto=None):
        self.inputs, self.layer, self.blocks = [whole] + ([] if onto is None else [onto]), layer, blocks
        self.listed, self.goes_on = range(blocks) if only is None else only, onto is not None
        dims = whole.shape[1:]
        self.outputs = [jax.ShapeDtypeStruct((8, *dims), whole.dtype)]
        self.scratch = [
            pltpu.VMEM(dims, whole.dtype),
            pltpu.SemaphoreType.DMA((2,)),
            pltpu.SemaphoreType.DMA((self.copies * blocks,)),
            pltpu.SemaphoreType.DMA((self.copies * blocks,)),
        ]

    def stage(self, at, number, ins, outs, scratch, c=0):
        (whole, *_), (full,), (held, local, *sems) = ins, outs, scratch
        own = whole.at[self.layer]
        rows = own.shape[0]
        width = own.shape[1] // self.blocks
        cols = pl.ds(c * width, width)
        low = 48 if rows == 160 else rows // 3
        both = rows - low
        everything = pl.ds(0, rows)
        plane = pl.ds(pl.multiple_of(at.z * low, 16), both)
        middle = pl.ds(low, both - low)
        mine = pl.ds(pl.multiple_of(at.z * both, 16), low)
        theirs = pl.ds(pl.multiple_of((1 - at.z) * both, 16), low)

        def copy(k):
            def again(s, r, peer):
                return full.at[s, r, cols], full.at[s, r, cols], peer

            src, dst, peer = {
                0: lambda: (own.at[plane, cols], full.at[at.s, plane, cols], at.to_x),
                1: lambda: (own.at[plane, cols], full.at[at.s, plane, cols], at.to_y),
                2: lambda: (own.at[everything, cols], full.at[at.s, everything, cols], at.to_sib),
                3: lambda: again(at.xs, middle, at.to_y),
                4: lambda: again(at.ys, mine, at.to_x),
                5: lambda: again(at.xs, mine, at.to_z),
                6: lambda: again(at.ys, mine, at.to_z),
                7: lambda: again(at.xs, plane, at.to_sib),
                8: lambda: again(at.ys, plane, at.to_sib),
                9: lambda: again(at.ds, mine, at.to_z),
                10: lambda: again(at.ds, plane, at.to_sib),
                11: lambda: again(at.xs, theirs, at.to_sib),
                12: lambda: again(at.ys, theirs, at.to_sib),
                13: lambda: again(at.ds, theirs, at.to_sib),
            }[k]()
            return remote(src, dst, sems, self.copies * c + k, peer)

        into = lambda: pltpu.make_async_copy(own, held, local.at[0])
        out = lambda: pltpu.make_async_copy(held, full.at[at.s], local.at[1])
        wait, start = {
            0: ((), (0, 1, 2)),
            1: ((0, 1), (3, 4, 5, 6, 7, 8)),
            2: ((3, 4), (9, 10)),
            3: ((5, 6, 9), (11, 12, 13)),
            4: ((2, 7, 8, 10, 11, 12, 13), ()),
        }[number]
        own_too = c == self.listed[0] and not self.goes_on
        if number == 1 and own_too:
            into().wait()
            out().start()
        for k in wait:
            copy(k).wait_recv()
        for k in start:
            copy(k).start()
        if number == 0 and own_too:
            into().start()
        if number == 4:
            for k in range(self.copies):
                copy(k).wait_send()
            if own_too:
                out().wait()


class Cross:
    blocks, last = 1, 1

    def __init__(self, part):
        self.inputs = [part]
        self.outputs = [jax.ShapeDtypeStruct(part.shape, BF)]
        self.scratch = [pltpu.SemaphoreType.DMA((2,)), pltpu.SemaphoreType.DMA((2,))]

    def pairs(self, at, ins, outs):
        (part,), (got,) = ins, outs
        half = part.shape[1] // 2
        low, high = pl.ds(0, half), pl.ds(half, half)
        return [(part.at[:, low, :], got.at[:, low, :], at.to_y), (part.at[:, high, :], got.at[:, high, :], at.to_x)]

    def stage(self, at, number, ins, outs, scratch, c=0):
        for k, (src, dst, peer) in enumerate(self.pairs(at, ins, outs)):
            copy = remote(src, dst, scratch, k, peer)
            if number == 0:
                copy.start()
            else:
                copy.wait()


class Rise(Cross):
    def pairs(self, at, ins, outs):
        (part,), (got,) = ins, outs
        return [(part, got, at.to_z)]


class Spread(Cross):
    def __init__(self, to_x, to_y):
        _, half, columns = to_x.shape
        self.inputs = [to_x, to_y]
        self.outputs = [jax.ShapeDtypeStruct((2, 2 * half, columns), BF)]
        self.scratch = [pltpu.SemaphoreType.DMA((2,)), pltpu.SemaphoreType.DMA((2,))]

    def pairs(self, at, ins, outs):
        (to_x, to_y), (got,) = ins, outs
        half = to_x.shape[1]
        return [(to_x, got.at[:, pl.ds(0, half), :], at.to_x), (to_y, got.at[:, pl.ds(half, half), :], at.to_y)]


class Chain:
    blocks, last = 2, 4

    def __init__(self, kept, to_x, to_y):
        _, rows, columns = kept.shape
        self.inputs = [kept, to_x, to_y]
        self.outputs = [jax.ShapeDtypeStruct((rows, columns), BF)]
        self.cut = columns // 2
        one, two = (2, rows, self.cut), (2, 2, rows, self.cut)
        self.scratch = [pltpu.VMEM(two, F32), pltpu.VMEM(two, BF)] + [pltpu.VMEM(one, BF)] * 4
        self.scratch += [pltpu.SemaphoreType.DMA((2, 5)), pltpu.SemaphoreType.DMA((2, 5)), pltpu.SemaphoreType.DMA((2, 2))]

    def stage(self, at, number, ins, outs, scratch, c=0):
        (kept, to_x, to_y), (result,), (base, far, ahead, second, sent, third, *sems, local) = ins, outs, scratch
        rows = kept.shape[1]
        half = rows // 2
        cols = pl.ds(c * self.cut, self.cut)
        low, high = pl.ds(0, half), pl.ds(half, half)

        def send(k):
            src, dst, peer = {
                0: lambda: (to_x.at[:, :, cols], far.at[c, :, low, :], at.to_x),
                1: lambda: (to_y.at[:, :, cols], far.at[c, :, high, :], at.to_y),
                2: lambda: (ahead.at[c, low, :], second.at[c, low, :], at.to_y),
                3: lambda: (ahead.at[c, high, :], second.at[c, high, :], at.to_x),
                4: lambda: (sent.at[c], third.at[c], at.to_z),
            }[k]()
            return pltpu.make_async_remote_copy(
                src_ref=src, dst_ref=dst, send_sem=sems[0].at[c, k], recv_sem=sems[1].at[c, k], device_id=peer, device_id_type=MESH
            )

        load = lambda: pltpu.make_async_copy(kept.at[:, :, cols], base.at[c], local.at[c, 0])
        store = lambda: pltpu.make_async_copy(sent.at[c], result.at[:, cols], local.at[c, 1])

        def each(f):
            @pl.loop(0, rows // 16)
            def _(k):
                f(pl.ds(pl.multiple_of(k * 16, 16), 16))

        if number == 0:
            for copy in (send(0), send(1), load()):
                copy.start()
        elif number == 1:
            for copy in (send(0), send(1), load()):
                copy.wait()

            def f(r):
                ahead[c, r, :] = (base[c, 1, r, :] + far[c, 1, r, :].astype(F32)).astype(BF)

            each(f)
            send(2).start()
            send(3).start()
        elif number == 2:
            send(2).wait()
            send(3).wait()

            def f(r):
                new = base[c, 0, r, :] + far[c, 0, r, :].astype(F32) + second[c, r, :].astype(F32)
                base[c, 0, r, :] = new
                sent[c, r, :] = new.astype(BF)

            each(f)
            send(4).start()
        elif number == 3:
            send(4).wait()

            def f(r):
                sent[c, r, :] = (base[c, 0, r, :] + third[c, r, :].astype(F32)).astype(BF)

            each(f)
            store().start()
        else:
            store().wait()


class Finish:
    last = 3

    def __init__(self, part, kept, far):
        mats, rows, columns = part.shape
        self.inputs = [part, kept, far]
        self.outputs = [jax.ShapeDtypeStruct(part.shape, BF)]
        self.blocks, self.cut = 2 * mats, columns // 2
        each = (self.blocks, rows, self.cut)
        n = self.blocks
        self.scratch = [pltpu.VMEM(each, F32)] + [pltpu.VMEM(each, BF)] * 4
        self.scratch += [pltpu.SemaphoreType.DMA((n, 3)), pltpu.SemaphoreType.DMA((n, 3)), pltpu.SemaphoreType.DMA((n, 3))]

    def stage(self, at, number, ins, outs, scratch, c=0):
        (part, kept, far), (result,), (total, first, second, sent, third, *sems, local) = ins, outs, scratch
        rows = part.shape[1]
        half = rows // 2
        m, cols = c // 2, pl.ds(c % 2 * self.cut, self.cut)
        low, high = pl.ds(0, half), pl.ds(half, half)

        def along(k):
            r, peer = ((low, at.to_y), (high, at.to_x))[k]
            return pltpu.make_async_remote_copy(
                src_ref=part.at[m, r, cols], dst_ref=second.at[c, r, :], send_sem=sems[0].at[c, k], recv_sem=sems[1].at[c, k],
                device_id=peer, device_id_type=MESH,
            )

        def up():
            return pltpu.make_async_remote_copy(
                src_ref=sent.at[c], dst_ref=third.at[c], send_sem=sems[0].at[c, 2], recv_sem=sems[1].at[c, 2],
                device_id=at.to_z, device_id_type=MESH,
            )

        def loads():
            return [
                pltpu.make_async_copy(kept.at[0, m, :, cols], total.at[c], local.at[c, 0]),
                pltpu.make_async_copy(far.at[0, m, :, cols], first.at[c], local.at[c, 1]),
            ]

        def store():
            return pltpu.make_async_copy(sent.at[c], result.at[m, :, cols], local.at[c, 2])

        def each(f):
            @pl.loop(0, rows // 16)
            def _(k):
                f(pl.ds(pl.multiple_of(k * 16, 16), 16))

        if number == 0:
            for copy in (along(0), along(1), *loads()):
                copy.start()
        elif number == 1:
            for copy in (along(0), along(1), *loads()):
                copy.wait()

            def f(r):
                new = total[c, r, :] + first[c, r, :].astype(F32) + second[c, r, :].astype(F32)
                total[c, r, :] = new
                sent[c, r, :] = new.astype(BF)

            each(f)
            up().start()
        elif number == 2:
            up().wait()

            def f(r):
                sent[c, r, :] = (total[c, r, :] + third[c, r, :].astype(F32)).astype(BF)

            each(f)
            store().start()
        else:
            store().wait()


def call(name, body, grid, ins, in_specs, outs, out_specs, scratch, comms, number, flops, points=None):
    n_in, n_out, n_scratch = len(ins), len(outs), len(scratch)
    steps = functools.reduce(lambda a, b: a * b, grid, 1)
    points = points or {}
    events = {}
    for index, m in enumerate(comms):
        for c in getattr(m, 'listed', range(m.blocks)):
            for stage in range(m.last + 1):
                when = points.get((index, c, stage), 0 if stage == 0 else steps)
                when = when if isinstance(when, tuple) else (when, 0)
                events.setdefault(when if when[0] < steps else END, []).append((stage == 0, c, stage, index))

    def kernel(*refs):
        refs = list(refs)
        take = lambda n: [refs.pop(0) for _ in range(n)]
        i_refs = take(n_in)
        ci = [take(len(m.inputs)) for m in comms]
        o_refs = take(n_out)
        co = [take(len(m.outputs)) for m in comms]
        s_refs = take(n_scratch)
        cs = [take(len(m.scratch)) for m in comms]
        at = Place()
        step = pl.program_id(0)
        if len(grid) == 2:
            step = step * grid[1] + pl.program_id(1)

        @pl.when(step == 0)
        def _():
            at.greet()

        def happen(sub):
            for when, listed in events.items():
                if when[1] == sub:
                    order = sorted(listed, key=lambda e: (e[2], e[1], e[3])) if when == END else sorted(listed)

                    @pl.when(step == (steps - 1 if when == END else when[0]))
                    def _(order=order):
                        for _, c, stage, index in order:
                            comms[index].stage(at, stage, ci[index], co[index], cs[index], c)

        happen(0)
        body(at, step, i_refs, o_refs, s_refs, (co, happen))
        happen(END[1])

    flat = lambda key: [v for m in comms for v in getattr(m, key)]
    moved = flat("inputs")
    aliases, i, o = {}, n_in, n_out
    for m in comms:
        if getattr(m, "goes_on", False):
            aliases[i + 1] = o
        i, o = i + len(m.inputs), o + len(m.outputs)
    results = pl.pallas_call(
        kernel,
        grid=grid,
        in_specs=list(in_specs) + [ANY] * len(moved),
        out_specs=list(out_specs) + [ANY] * len(flat("outputs")),
        out_shape=list(outs) + flat("outputs"),
        scratch_shapes=list(scratch) + flat("scratch"),
        compiler_params=pltpu.CompilerParams(
            collective_id=number,
            has_side_effects=True,
            vmem_limit_bytes=VMEM_LIMIT,
            dimension_semantics=("arbitrary",) * len(grid),
        ),
        cost_estimate=pl.CostEstimate(flops=flops, bytes_accessed=1 << 24, transcendentals=0),
        name=name,
        input_output_aliases=aliases,
    )(*ins, *moved)
    results = list(results)
    mine, results = results[:n_out], results[n_out:]
    got = []
    for m in comms:
        got.append(results[: len(m.outputs)])
        results = results[len(m.outputs) :]
    return mine, got


def scale_of(wide):
    return lax.rsqrt(jnp.mean(wide * wide, -1, keepdims=True) + 1e-6)


def shape(dims, dtype=BF):
    return jax.ShapeDtypeStruct(dims, dtype)


def once(dims, index):
    return pl.BlockSpec(dims, index, pipeline_mode=pl.Buffered(1))


def dot(a, b, ca=1, cb=0):
    return lax.dot_general(a, b, (((ca,), (cb,)), ((), ())), preferred_element_type=F32)


def load_block(landed, buffers, sems, c, width):
    cols = pl.ds(c * width if isinstance(c, int) else pl.multiple_of(c * width, width), width)
    return [pltpu.make_async_copy(landed[m][0].at[:, :, cols], buffers.at[c % 2, m], sems.at[c % 2, m]) for m in range(2)]


def gate_up(x, w_gate, w_up, w_down, number):
    cols, blocks, lag = 512, FF // 512, 5

    def body(at, step, ins, outs, scratch, landed):
        x_ref = ins[0]
        a_out, act, gate, up = outs
        held, sems = scratch

        @pl.when(step == 0)
        def _():
            for k in range(TOK // 512):
                part = pl.ds(k * 512, 512)
                wide = x_ref[part, :].astype(F32)
                a_out[part, :] = (wide * scale_of(wide)).astype(BF)

        def load(c):
            for copy in load_block(arrived, held, sems, c, cols):
                copy.start()

        arrived, happen = landed

        @pl.when(step == lag - 1)
        def _():
            load(0)

        c = jnp.maximum(step - lag, 0)

        @pl.when(step >= lag)
        def _():
            for copy in load_block(arrived, held, sems, c, cols):
                copy.wait()

        for k in range(4):
            if k:
                happen(k)
            if k == 3:

                @pl.when((step >= lag) & (step < lag + blocks - 1))
                def _():
                    load(c + 1)

            @pl.when(step >= lag)
            def _(k=k):
                part = pl.ds(k * 512, 512)
                left = a_out[part, :]
                g = dot(left, held[c % 2, 0].reshape(D, cols))
                u = dot(left, held[c % 2, 1].reshape(D, cols))
                gate[part, :] = g
                up[part, :] = u
                act[part, :] = (g * jax.nn.sigmoid(g) * u).astype(BF)

    tile = pl.BlockSpec((TOK, cols), lambda i: (0, jnp.maximum(i - lag, 0)))
    whole = once((TOK, D), lambda i: (0, 0))
    comms = [Gather(w_gate, 0, blocks), Gather(w_up, 0, blocks), Gather(w_down, 0, 2)]
    when = {(0, k): k for k in range(5)} | {(1, 0): 1, (1, 1): lag - 1, (2, 0): lag - 1}
    for c in range(1, blocks + 1):
        rest = {(c + 1, 0): (lag + c - 2, 2), (c, 1): (lag + c - 2, 2), (c, 2): lag + c - 1, (c, 3): (lag + c - 1, 2), (c, 4): (lag + c - 1, 3)}
        when = rest | when
    points = {(m, c, k): when[c, k] for m in range(2) for c in range(blocks) for k in range(5)}
    points |= {(2, c, k): when[blocks - 1 + c, k] for c in range(2) for k in range(4)}
    return call(
        "gate_up", body, (blocks + lag,), [x], [whole], [shape((TOK, D)), shape((TOK, FF)), shape((TOK, FF), F32), shape((TOK, FF), F32)],
        [whole, tile, tile, tile], [pltpu.VMEM((2, 2, 8, 160, cols), BF), pltpu.SemaphoreType.DMA((2, 2))], comms, number, 4 * TOK * D * FF, points,
    )


def down(act, wd, h, comms, number, points):
    rows = 256

    def body(at, step, ins, outs, scratch, landed):
        act_ref, w_ref, h_ref = ins
        out = dot(act_ref[...], w_ref[...].reshape(FF, D)).astype(BF)
        new = (h_ref[...].astype(F32) + out.astype(F32)).astype(BF)
        outs[0][...] = new
        wide = new.astype(F32)
        outs[1][...] = (wide * scale_of(wide)).astype(BF)

    tile = pl.BlockSpec((rows, D), lambda i: (i, 0))
    return call(
        "down", body, (TOK // rows,), [act, wd, h], [pl.BlockSpec((rows, FF), lambda i: (i, 0)), once((8, 384, D), lambda i: (0, 0, 0)), tile],
        [shape((TOK, D)), shape((TOK, D))], [tile, tile], [], comms, number, 2 * TOK * D * FF, points,
    )


def middle(a, dy, wd, saved, weights, comms, number, extra=None):
    cols, rows = 768, 512
    blocks, tiles, n = FF // cols, TOK // rows, 2 * (FF // cols)
    lead = 1 if weights else 0
    steps = lead + blocks * tiles + 1
    across = TOK // tiles

    def body(at, step, ins, outs, scratch, landed):
        a_ref, dy_ref, wd_ref, *ins = ins
        d_out, kept, far, *outs = outs
        d_all, term, mine, send, recv, to_x, to_y, *sems = scratch
        t = step - lead
        j, i = t // tiles, t % tiles
        arrived, happen = landed

        def copy(u):
            return remote(send.at[u % 2], recv.at[u % 4], [s for s in sems[0:2]], u, at.to_sib)

        def there(u, half):
            return far.at[:, u % 2, pl.ds(80 * half, 80), pl.ds(pl.multiple_of(u // 2 * cols, cols), cols)]

        def along_x(u):
            return remote(to_x.at[u % 2], there(u, 0), sems[2:4], u, at.to_x)

        def along_y(u):
            return remote(to_y.at[u % 2], there(u, 1), sems[4:6], u, at.to_y)

        def finish(u):
            @pl.when(u > 1)
            def _():
                along_x(u - 2).wait_send()
                along_y(u - 2).wait_send()

            copy(u).wait_recv()
            slot = u % 2
            total = [mine[slot, k].astype(F32) + recv[u % 4, k].astype(F32) for k in range(4)]
            to_x[slot, 0] = total[0][:80].astype(BF)
            to_x[slot, 1] = total[1][:80].astype(BF)
            to_y[slot, 0] = total[2][80:].astype(BF)
            to_y[slot, 1] = total[1][80:].astype(BF)
            kept[0, 0] = total[3]
            kept[1, 0, :80] = total[2][:80]
            kept[1, 0, 80:] = total[0][80:]
            along_x(u).start()
            along_y(u).start()

        if weights:
            held, loads = scratch[-2:]

            @pl.when(step == lead - 1)
            def _():
                for load in load_block(arrived, held, loads, 0, cols):
                    load.start()

            @pl.when((t >= 0) & (t < blocks * tiles) & (i == 0))
            def _():
                for load in load_block(arrived, held, loads, j, cols):
                    load.wait()

        @pl.when((t >= 0) & (t < blocks * tiles))
        def _():
            sub = 256
            w = wd_ref[...].reshape(cols, D)
            for k in range(rows // sub):
                here = pl.ds(k * sub, sub)
                if weights:
                    left = a_ref[pl.ds(pl.multiple_of(i * rows + k * sub, sub), sub), :]
                    g = dot(left, held[j % 2, 0].reshape(D, cols))
                    u = dot(left, held[j % 2, 1].reshape(D, cols))
                else:
                    g, u = ins[0][here, :], ins[1][here, :]
                da = dot(dy_ref[here, :], w, 1, 1).astype(BF).astype(F32)
                sig = jax.nn.sigmoid(g)
                silu = g * sig
                if weights:
                    outs[0][here, :] = (silu * u).astype(BF)
                d_gate = (da * u * (sig + silu * (1 - sig))).astype(BF)
                d_up = (da * silu).astype(BF)
                d_out[0, here, :] = d_gate
                d_out[1, here, :] = d_up
                to = pl.ds(pl.multiple_of(i * rows + k * sub, sub), sub)
                d_all[0, to, :] = d_gate
                d_all[1, to, :] = d_up

        @pl.when((t > 0) & (i == 0))
        def _():
            finish(2 * j - 1)

        happen(1)

        for m in range(2):
            if m:
                happen(2)

            @pl.when((t >= 0) & (t < blocks * tiles) & (i == tiles - 1))
            def _(m=m):
                u = 2 * j + m

                @pl.when(u > 1)
                def _():
                    copy(u - 2).wait_send()

                term[...] = dot(a_ref[...], d_all[m], 0, 0).astype(BF).reshape(8, 160, cols)
                for k in range(4):
                    send[m, k] = term[2 * place(at, k) + 1 - at.c]
                    mine[m, k] = term[2 * place(at, k) + at.c]
                copy(u).start()
                if m:
                    finish(2 * j)

        happen(3)
        if weights:

            @pl.when((t >= 0) & (t < (blocks - 1) * tiles) & (i == tiles - 1))
            def _():
                for load in load_block(arrived, held, loads, j + 1, cols):
                    load.start()

        @pl.when(step == steps - 1)
        def _():
            for u in (n - 2, n - 1):
                copy(u).wait_send()
                along_x(u).wait_send()
                along_y(u).wait_send()

            @pl.loop(0, n)
            def _(u):
                along_x(u).wait_recv()
                along_y(u).wait_recv()

    def block(s):
        t = jnp.clip(s - lead, 0, blocks * tiles - 1)
        return t // tiles, t % tiles

    def done(s):
        t = jnp.maximum(s - lead, 0)
        late = t % tiles == tiles - 1
        early = t < tiles - 1
        return 0, jnp.where(late | early, 0, 1), 0, jnp.where(late, t // tiles, jnp.maximum(t // tiles - 1, 0))

    tile = pl.BlockSpec((rows, cols), lambda s: (block(s)[1], block(s)[0]))
    sems = lambda: pltpu.SemaphoreType.DMA((n,))
    ins = [a, dy, wd] + (list(saved) if saved else [])
    in_specs = [once((TOK, D), lambda s: (0, 0)), pl.BlockSpec((rows, D), lambda s: (block(s)[1], 0)), pl.BlockSpec((2, 384, D), lambda s: (block(s)[0], 0, 0))]
    in_specs += [tile, tile] if saved else []
    scratch = [
        pltpu.VMEM((2, TOK, cols), BF), pltpu.VMEM((8, 160, cols), BF), pltpu.VMEM((2, 4, 160, cols), BF), pltpu.VMEM((2, 4, 160, cols), BF),
        pltpu.VMEM((4, 4, 160, cols), BF), pltpu.VMEM((2, 2, 80, cols), BF), pltpu.VMEM((2, 2, 80, cols), BF),
    ] + [sems() for _ in range(6)]
    points = extra
    if weights:
        comms = [Gather(w, 1, blocks, (1, 2, 3), begun) for w, begun in weights] + comms
        scratch += [pltpu.VMEM((2, 2, 8, 160, cols), BF), pltpu.SemaphoreType.DMA((2, 2))]
        when = {1: (0, 4, (4, 2), (4, 3), (4, 3)), 2: (0, (4, 2), 5, 6, 7), 3: ((4, 2), 7, 8, (8, 1), (8, 2))}
        points = {(m, c, k): when[c][k] for m in range(2) for c in when for k in range(5)}
    outs = [shape((2, TOK, FF)), shape((2, 2, 160, FF), F32), shape((2, 2, 160, FF))] + ([shape((TOK, FF))] if weights else [])
    out_specs = [
        pl.BlockSpec((2, rows, cols), lambda s: (0, block(s)[1], block(s)[0])), pl.BlockSpec((2, 1, 160, cols), done), ANY,
    ] + ([tile] if weights else [])
    (dgu, kept, far, *act), got = call(
        "middle", body, (steps,), ins, in_specs, outs, out_specs, scratch, comms, number, (10 if weights else 6) * TOK * D * FF, points,
    )
    return dgu, Sum(kept, far), act, got


def by_state(dgu, wg, wu, h, dy, comms, number, points=None):
    rows = 256

    def body(at, step, ins, outs, scratch, landed):
        d_ref, g_ref, u_ref, h_ref, dy_ref = ins
        first = dot(d_ref[0], g_ref[...].reshape(D, FF), 1, 1).astype(BF)
        second = dot(d_ref[1], u_ref[...].reshape(D, FF), 1, 1).astype(BF)
        da = (first.astype(F32) + second.astype(F32)).astype(BF).astype(F32)
        wide = h_ref[...].astype(F32)
        scale = scale_of(wide)
        along = jnp.sum(da * wide, -1, keepdims=True)
        dh = da * scale - wide * (along * scale * scale * scale * (1.0 / D))
        outs[0][...] = (dy_ref[...].astype(F32) + dh.astype(BF).astype(F32)).astype(BF)

    tile = pl.BlockSpec((rows, D), lambda i: (i, 0))
    weight = once((8, 160, FF), lambda i: (0, 0, 0))
    return call(
        "by_state", body, (TOK // rows,), [dgu, wg, wu, h, dy],
        [pl.BlockSpec((2, rows, FF), lambda i: (0, i, 0)), weight, weight, tile, tile],
        [shape((TOK, D))], [tile], [], comms, number, 4 * TOK * D * FF, points,
    )


def place(at, k):
    return (at.x + (1 - 2 * at.x if k < 2 else 0)) * 2 + at.y + (1 - 2 * at.y if k in (1, 2) else 0)


def by_down(act, dy, comms, number):
    n = 4
    low, high = slice(0, 192), slice(192, 384)
    flows = ((1, 1), (1, 0), (0, 1), (0, 0))
    slots = ((1, 1), (0, None), (None, 0), (None, None))

    def body(at, step, ins, outs, scratch, landed):
        act_ref, dy_ref = ins
        kept, to_x, to_y = outs
        mine, send, recv, *sems = scratch

        def copy(t):
            return remote(send.at[t % 2], recv.at[t], sems[0:2], t, at.to_sib)

        @pl.when(step > 1)
        def _():
            copy(step - 2).wait_send()

        def product(core):
            half = act_ref[:, pl.ds(pl.multiple_of(core * 384, 128), 384)]
            return dot(half, dy_ref[...], 0, 0).astype(BF)

        send[step % 2] = product(1 - at.c)
        copy(step).start()
        mine[...] = product(at.c)

        for t in range(n):

            @pl.when(step == t)
            def _(t=t):
                copy(t).wait_recv()
                total = mine[...].astype(F32) + recv[t].astype(F32)
                a, b = total[low], total[high]
                if flows[t][0]:
                    to_x[slots[t][0]] = a.astype(BF)
                else:
                    kept[1 if flows[t][1] else 0, low, :] = a
                if flows[t][1]:
                    to_y[slots[t][1]] = b.astype(BF)
                else:
                    kept[1 if flows[t][0] else 0, high, :] = b

        @pl.when(step == n - 1)
        def _():
            copy(n - 2).wait_send()
            copy(n - 1).wait_send()

    def now(i):
        at = Place()
        fx, fy = 1 - i // 2, 1 - i % 2
        return 0, (at.x + fx * (1 - 2 * at.x)) * 2 + at.y + fy * (1 - 2 * at.y)

    whole = lambda *dims: pl.BlockSpec(dims, lambda i: (0,) * len(dims))
    return call(
        "by_down", body, (n,), [act, dy],
        [pl.BlockSpec((TOK, 768), now), once((TOK, D), lambda i: (0, 0))],
        [shape((2, 384, D), F32), shape((2, 192, D)), shape((2, 192, D))], [whole(2, 384, D), whole(2, 192, D), whole(2, 192, D)],
        [pltpu.VMEM((384, D), BF), pltpu.VMEM((2, 384, D), BF), pltpu.VMEM((n, 384, D), BF)] + [pltpu.SemaphoreType.DMA((n,)) for _ in range(2)],
        comms, number, 2 * TOK * D * FF,
    )


class Sum:
    def __init__(self, kept, far):
        self.kept, self.far = kept, far

    def next(self):
        return (self.kept[1] + self.far[1].astype(F32)).astype(BF)

    def cross(self):
        return Cross(self.next())

    def finish(self):
        return Finish(self.next(), self.kept, self.far)

    def rise(self, got):
        self.total = self.kept[0] + self.far[0].astype(F32) + got.astype(F32)
        return self.total.astype(BF)

    def end(self, got):
        return (self.total + got.astype(F32)).astype(BF)


def solution(mesh):
    def step(x, dy, w_gate, w_up, w_down):
        x, dy = x[0], dy[0]
        (a0, act0, gate0, up0), ((g0,), (u0,), (d0,)) = gate_up(x, w_gate, w_up, w_down, 0)
        early = [Gather(w_down, 1, 2), Gather(w_gate, 1, 4, (0,)), Gather(w_up, 1, 4, (0,))]
        when = {(0, 0, 1): 3, (0, 1, 1): 5, (0, 0, 2): 6, (1, 0, 0): 3, (2, 0, 0): 3, (1, 0, 1): 7, (2, 0, 1): 7, (0, 1, 2): 7}
        (h1, a1), ((d1,), (g1,), (u1,)) = down(act0, d0, x, early, 1, when)
        dgu1, s_gu1, (act1,), ((g1,), (u1,)) = middle(a1, dy, d1, None, ((w_gate, g1), (w_up, u1)), [], 2)
        (kept, *parts), _ = by_down(act1, dy, [], 3)
        (dh1,), ((got,), (far,)) = by_state(dgu1, g1, u1, h1, dy, [s_gu1.cross(), Spread(*parts)], 4)
        s_d1 = Sum(kept[:, None], far[:, None])
        (kept, *parts), ((got_d1,),) = by_down(act0, dh1, [s_d1.cross()], 5)
        comms = [Chain(kept, *parts), Rise(s_gu1.rise(got)), Rise(s_d1.rise(got_d1))]
        end_d0 = {(0, c, k): when for c in range(2) for k, when in ((1, 6), (2, 10), (3, 15))}
        dgu0, s_gu0, _, ((down0,), (z_gu1,), (z_d1,)) = middle(a0, dh1, d0, (gate0, up0), None, comms, 6, end_d0)
        end_gu0 = {(0, 0, 1): 1, (0, 1, 1): 2, (0, 2, 1): 3, (0, 3, 1): 4, (0, 0, 2): 4, (0, 1, 2): 6, (0, 2, 2): 7}
        (dx,), ((gu0,),) = by_state(dgu0, g0, u0, x, dh1, [s_gu0.finish()], 7, end_gu0)

        gu1, down1 = s_gu1.end(z_gu1), s_d1.end(z_d1)
        return dx[None], jnp.stack([gu0[0], gu1[0]]), jnp.stack([gu0[1], gu1[1]]), jnp.stack([down0, down1[0]])

    states, cut = P(("rep", "r", "s"), None, None), P(None, "s", None)
    return jax.shard_map(
        step,
        mesh=mesh,
        in_specs=(states, states) + (cut,) * 3,
        out_specs=(states,) + (P("rep", "s", None),) * 3,
        check_vma=False,
    )
```

time: 954 us -> 637 us (0.67)
  Pallas kernels: 0 us -> 592 us
  matrix products: 452 us -> 0 us
  waiting for transfers between devices: 414 us -> 0 us
  local copies, waits for them, and re-layouts: 32.2 us -> 6.98 us
  between operations: 14.3 us -> 1.24 us
    pallas_call x0 -> x8, Pallas kernels: none -> 592 us  [call(): pl.pallas_call(kernel, grid=grid, in_specs=list(in_specs) + [ANY] * len(m...]
    dot_general x17 -> x0, matrix products: 452 us -> none  [the longest x6 164 us: layer(): up = jnp.dot(a, w['w_up'], preferred_element_type=jnp.float32)]
    reduce_scatter x6 -> x0, waiting for transfers between devices: 172 us -> none  [summed(): lax.psum_scatter(term, 's', scatter_dimension=0, tiled=True)]
    all_gather x6 -> x0, waiting for transfers between devices: 146 us -> none  [fetched(): lax.all_gather(w[number], 's', axis=0, tiled=True)]
    psum x1 -> x0, waiting for transfers between devices: 94.1 us -> none  [summed(): lax.psum(lax.psum_scatter(term, 's', scatter_dimension=0, tiled=True), 'r')]
    convert_element_type x0 -> x7, other arithmetic: none -> 24.7 us  [the longest x3 9.36 us: next(): return (self.kept[1] + self.far[1].astype(F32)).astype(BF)]
    unnamed x27 -> x23, local copies, waits for them, and re-layouts: 24.9 us -> 4.13 us
    broadcast_in_dim x1 -> x0, other arithmetic: 12.3 us -> none  [step(): by_h[None]]
  transfers between devices with their start and end apart: 13 -> 0, of which waited for: 10 -> 0; matrix products, arithmetic and copies ran while one was open for 46% -> 0% of each run, Pallas kernels for 0% -> 0%
where the time goes in v2:
time: 637 us; the launch traced here: 629 us
  Pallas kernels  592 us (93%)
  other arithmetic  28.4 us (4%)
  local copies, waits for them, and re-layouts  6.98 us (1%)
    pallas_call x8, Pallas kernels, call(): pl.pallas_call(kernel, grid=grid, in_specs=list(in_specs) + [ANY] * len(m...  592 us

profile of v2, /device:TPU:0, one launch (start us, length us, event | category | flops | bytes accessed | tf_op | source)
XLA Modules:
  0.0 628.7 jit_solution(544902849214411498)
XLA Ops:
  0.6 100.8 %gate_up.1 = (bf16[2048,1280]{1,0:T(8,128)(2,1)}, bf16[2048,3072]{1,0:T(8,128)(2,1)}, f32[2048,3072]{1,0:T(8,128)}, f32[2048,3072]{1,0:T(8,128)}, bf16[8,160,307...) custom-call(bf16[2048,1280]{1,0:T(8,128)(2,1)} %bitcast.23, ...), custom_call_target="tpu_custom_call" | custom-call | flops 32212254720 | bytes 16777216 | tf_op jit(solution)/shard_map/gate_up/pallas_call | solution.py:364
  101.4 50.7 %down.1 = (bf16[2048,1280]{1,0:T(8,128)(2,1)}, bf16[2048,1280]{1,0:T(8,128)(2,1)}, bf16[8,384,1280]{2,1,0:T(8,128)(2,1)}, bf16[8,160,3072]{2,1,0:T(8,128)(2,1)}, bf16[8,160,3072]{2,1,0:T(8,128)(2,1)}) custom-call(bf16[2048,3072]{1,0:T(8,128)(2,1)} %get-tuple-element.41.refs_0_, bf16[8,384,1280]{2,1,0:T(8,128)(2,1)} %get-tuple-element.42.refs_1_.refs_2_, ...), custom_call_target="tpu_custom_call" | custom-call | flops 16106127360 | bytes 16777216 | tf_op jit(solution)/shard_map/down/pallas_call | solution.py:364
  152.1 151.1 %middle.2 = (bf16[2,2048,3072]{2,1,0:T(8,128)(2,1)}, f32[2,2,160,3072]{3,2,1,0:T(8,128)}, bf16[2,2,160,3072]{3,2,1,0:T(8,128)(2,1)}, bf16[2048,3072]{1,0:T(8,128...) custom-call(bf16[2048,1280]{1,0:T(8,128)(2,1)} %get-tuple-element.43, ...), custom_call_target="tpu_custom_call", output_to_operand_aliasing={{4}: (4, {}), {5}: (6, {})} | custom-call | flops 80530636800 | bytes 16777216 | tf_op jit(solution)/shard_map/middle/pallas_call | solution.py:364
  303.2 4.6 fusion.refs_5_
  307.8 29.4 %by_down.2 = (f32[2,384,1280]{2,1,0:T(8,128)}, bf16[2,192,1280]{2,1,0:T(8,128)(2,1)}, bf16[2,192,1280]{2,1,0:T(8,128)(2,1)}) custom-call(bf16[2048,3072]{1,0:T(8,128)(2,1)} %get-tuple-element.53.refs_0_, bf16[2048,1280]{1,0:T(8,128)(2,1)} %bitcast.21), custom_call_target="tpu_custom_call" | custom-call | flops 16106127360 | bytes 16777216 | tf_op jit(solution)/shard_map/by_down/pallas_call | solution.py:364
  337.1 52.5 %by_state.2 = (bf16[2048,1280]{1,0:T(8,128)(2,1)}, bf16[2,160,3072]{2,1,0:T(8,128)(2,1)}, bf16[2,384,1280]{2,1,0:T(8,128)(2,1)}) custom-call(bf16[2,2048,3072]{2,1,0:T(8,128)(2,1)} %get-tuple-element.47.refs_0_, bf16[8,160,3072]{2,1,0:T(8,128)(2,1)} %get-tuple-element.48.refs_1_, bf16[8,160,3072]{2,1,0:T(8,128)(2,1)} %get-tuple-element.49.refs_2_, ...), custom_call_target="tpu_custom_call" | custom-call | flops 32212254720 | bytes 16777216 | tf_op jit(solution)/shard_map/by_state/pallas_call | solution.py:364
  389.6 2.9 add_convert_fusion.4.refs_2_
  392.5 29.6 %by_down.3 = (f32[2,384,1280]{2,1,0:T(8,128)}, bf16[2,192,1280]{2,1,0:T(8,128)(2,1)}, bf16[2,192,1280]{2,1,0:T(8,128)(2,1)}, bf16[1,384,1280]{2,1,0:T(8,128)(2,1)}) custom-call(bf16[2048,3072]{1,0:T(8,128)(2,1)} %get-tuple-element.41.refs_0_, bf16[2048,1280]{1,0:T(8,128)(2,1)} %get-tuple-element.56.refs_1_.refs_4_, ...), custom_call_target="tpu_custom_call" | custom-call | flops 16106127360 | bytes 16777216 | tf_op jit(solution)/shard_map/by_down/pallas_call | solution.py:364
  422.1 3.5 fusion.3.refs_9_
  425.6 4.9 fusion.2.refs_8_
  430.5 118.7 %middle.3 = (bf16[2,2048,3072]{2,1,0:T(8,128)(2,1)}, f32[2,2,160,3072]{3,2,1,0:T(8,128)}, bf16[2,2,160,3072]{3,2,1,0:T(8,128)(2,1)}, bf16[384,1280]{1,0:T(8,128)...) custom-call(bf16[2048,1280]{1,0:T(8,128)(2,1)} %get-tuple-element.40.refs_0_, ...), custom_call_target="tpu_custom_call" | custom-call | flops 48318382080 | bytes 16777216 | tf_op jit(solution)/shard_map/middle/pallas_call | solution.py:364
  549.2 2.8 add_convert_fusion.3
  552.0 0.0 slice-start.2
  552.0 0.5 copy-done.1
  552.5 0.6 copy-done.2
  553.1 4.2 add_convert_fusion
  557.3 0.0 copy-start.6
  557.3 0.0 copy-start.5
  557.3 1.1 fusion.5
  558.4 0.4 copy-done.6
  558.8 1.4 pad_maximum_fusion.2
  560.2 0.0 slice-done.2
  560.2 0.1 copy-done.5
  560.3 1.9 fusion.1.refs_5_
  562.2 59.5 %by_state.3 = (bf16[2048,1280]{1,0:T(8,128)(2,1)}, bf16[2,160,3072]{2,1,0:T(8,128)(2,1)}) custom-call(bf16[2,2048,3072]{2,1,0:T(8,128)(2,1)} %get-tuple-element.66.refs_0_, bf16[8,160,3072]{2,1,0:T(8,128)(2,1)} %get-tuple-element.67.refs_1_, bf16[8,160,3072]{2,1,0:T(8,128)(2,1)} %get-tuple-element.68.refs_2_, bf16[2048,1280]{1,0:T(8,128)(2,1)} %bitcast.25, ...), custom_call_target="tpu_custom_call" | custom-call | flops 32212254720 | bytes 16777216 | tf_op jit(solution)/shard_map/by_state/pallas_call | solution.py:364
  621.7 0.0 copy-start.4
  621.7 0.0 slice-start
  621.7 1.8 fusion.4
  623.5 0.0 slice-start.1
  623.5 2.3 pad_maximum_fusion
  625.8 0.1 slice-done.1
  625.9 2.4 copy.14
  (12 shorter events, 0.0 us)
Async XLA Ops:
  422.1 3.5 copy-start
  430.5 118.7 %copy-start.3 = (bf16[1,384,1280]{2,1,0:T(8,128)(2,1)S(1)}, bf16[1,384,1280]{2,1,0:T(8,128)(2,1)}, u32[]{:S(2)}) copy-start(bf16[1,384,1280]{2,1,0:T(8,128)(2,1)} %get-tuple-element.65) | copy-start | bytes 2949124
  549.2 3.3 copy-start.1
  549.2 3.9 copy-start.2
  552.0 8.3 %slice-start.2 = ((s8[7864320]{0:T(1024)(128)(4,1)}), s8[4194304]{0:T(1024)(128)(4,1)S(1)}, s32[]{:S(2)}) async-start(s8[7864320]{0:T(1024)(128)(4,1)} %bitcast.17), calls=%async_computation.2 | async-start | bytes 8388608
  553.1 7.1 %slice-start.3 = ((s8[7864320]{0:T(1024)(128)(4,1)}), s8[3670016]{0:T(1024)(128)(4,1)S(1)}, s32[]{:S(2)}) async-start(s8[7864320]{0:T(1024)(128)(4,1)} %bitcast.17), calls=%async_computation.3 | async-start | bytes 7340032
  557.3 1.5 copy-start.6
  557.3 3.0 copy-start.5
  621.7 1.8 copy-start.4
  621.7 4.1 slice-start
  623.5 2.4 slice-start.1

commit v3 on v2

--- a/solution.py
+++ b/solution.py
@@ -46,9 +46,8 @@
     copies = 14
     last = 4
 
-    def __init__(self, whole, layer, blocks=1, only=None, onto=None):
-        self.inputs, self.layer, self.blocks = [whole] + ([] if onto is None else [onto]), layer, blocks
-        self.listed, self.goes_on = range(blocks) if only is None else only, onto is not None
+    def __init__(self, whole, layer, blocks=1):
+        self.inputs, self.layer, self.blocks = [whole], layer, blocks
         dims = whole.shape[1:]
         self.outputs = [jax.ShapeDtypeStruct((8, *dims), whole.dtype)]
         self.scratch = [
@@ -59,7 +58,7 @@
         ]
 
     def stage(self, at, number, ins, outs, scratch, c=0):
-        (whole, *_), (full,), (held, local, *sems) = ins, outs, scratch
+        (whole,), (full,), (held, local, *sems) = ins, outs, scratch
         own = whole.at[self.layer]
         rows = own.shape[0]
         width = own.shape[1] // self.blocks
@@ -103,20 +102,19 @@
             3: ((5, 6, 9), (11, 12, 13)),
             4: ((2, 7, 8, 10, 11, 12, 13), ()),
         }[number]
-        own_too = c == self.listed[0] and not self.goes_on
-        if number == 1 and own_too:
+        if number == 1 and c == 0:
             into().wait()
             out().start()
         for k in wait:
             copy(k).wait_recv()
         for k in start:
             copy(k).start()
-        if number == 0 and own_too:
+        if number == 0 and c == 0:
             into().start()
         if number == 4:
             for k in range(self.copies):
                 copy(k).wait_send()
-            if own_too:
+            if c == 0:
                 out().wait()
 
 
@@ -147,94 +145,6 @@
     def pairs(self, at, ins, outs):
         (part,), (got,) = ins, outs
         return [(part, got, at.to_z)]
-
-
-class Spread(Cross):
-    def __init__(self, to_x, to_y):
-        _, half, columns = to_x.shape
-        self.inputs = [to_x, to_y]
-        self.outputs = [jax.ShapeDtypeStruct((2, 2 * half, columns), BF)]
-        self.scratch = [pltpu.SemaphoreType.DMA((2,)), pltpu.SemaphoreType.DMA((2,))]
-
-    def pairs(self, at, ins, outs):
-        (to_x, to_y), (got,) = ins, outs
-        half = to_x.shape[1]
-        return [(to_x, got.at[:, pl.ds(0, half), :], at.to_x), (to_y, got.at[:, pl.ds(half, half), :], at.to_y)]
-
-
-class Chain:
-    blocks, last = 2, 4
-
-    def __init__(self, kept, to_x, to_y):
-        _, rows, columns = kept.shape
-        self.inputs = [kept, to_x, to_y]
-        self.outputs = [jax.ShapeDtypeStruct((rows, columns), BF)]
-        self.cut = columns // 2
-        one, two = (2, rows, self.cut), (2, 2, rows, self.cut)
-        self.scratch = [pltpu.VMEM(two, F32), pltpu.VMEM(two, BF)] + [pltpu.VMEM(one, BF)] * 4
-        self.scratch += [pltpu.SemaphoreType.DMA((2, 5)), pltpu.SemaphoreType.DMA((2, 5)), pltpu.SemaphoreType.DMA((2, 2))]
-
-    def stage(self, at, number, ins, outs, scratch, c=0):
-        (kept, to_x, to_y), (result,), (base, far, ahead, second, sent, third, *sems, local) = ins, outs, scratch
-        rows = kept.shape[1]
-        half = rows // 2
-        cols = pl.ds(c * self.cut, self.cut)
-        low, high = pl.ds(0, half), pl.ds(half, half)
-
-        def send(k):
-            src, dst, peer = {
-                0: lambda: (to_x.at[:, :, cols], far.at[c, :, low, :], at.to_x),
-                1: lambda: (to_y.at[:, :, cols], far.at[c, :, high, :], at.to_y),
-                2: lambda: (ahead.at[c, low, :], second.at[c, low, :], at.to_y),
-                3: lambda: (ahead.at[c, high, :], second.at[c, high, :], at.to_x),
-                4: lambda: (sent.at[c], third.at[c], at.to_z),
-            }[k]()
-            return pltpu.make_async_remote_copy(
-                src_ref=src, dst_ref=dst, send_sem=sems[0].at[c, k], recv_sem=sems[1].at[c, k], device_id=peer, device_id_type=MESH
-            )
-
-        load = lambda: pltpu.make_async_copy(kept.at[:, :, cols], base.at[c], local.at[c, 0])
-        store = lambda: pltpu.make_async_copy(sent.at[c], result.at[:, cols], local.at[c, 1])
-
-        def each(f):
-            @pl.loop(0, rows // 16)
-            def _(k):
-                f(pl.ds(pl.multiple_of(k * 16, 16), 16))
-
-        if number == 0:
-            for copy in (send(0), send(1), load()):
-                copy.start()
-        elif number == 1:
-            for copy in (send(0), send(1), load()):
-                copy.wait()
-
-            def f(r):
-                ahead[c, r, :] = (base[c, 1, r, :] + far[c, 1, r, :].astype(F32)).astype(BF)
-
-            each(f)
-            send(2).start()
-            send(3).start()
-        elif number == 2:
-            send(2).wait()
-            send(3).wait()
-
-            def f(r):
-                new = base[c, 0, r, :] + far[c, 0, r, :].astype(F32) + second[c, r, :].astype(F32)
-                base[c, 0, r, :] = new
-                sent[c, r, :] = new.astype(BF)
-
-            each(f)
-            send(4).start()
-        elif number == 3:
-            send(4).wait()
-
-            def f(r):
-                sent[c, r, :] = (base[c, 0, r, :] + third[c, r, :].astype(F32)).astype(BF)
-
-            each(f)
-            store().start()
-        else:
-            store().wait()
 
 
 class Finish:
@@ -316,7 +226,7 @@
     points = points or {}
     events = {}
     for index, m in enumerate(comms):
-        for c in getattr(m, 'listed', range(m.blocks)):
+        for c in range(m.blocks):
             for stage in range(m.last + 1):
                 when = points.get((index, c, stage), 0 if stage == 0 else steps)
                 when = when if isinstance(when, tuple) else (when, 0)
@@ -356,11 +266,6 @@
 
     flat = lambda key: [v for m in comms for v in getattr(m, key)]
     moved = flat("inputs")
-    aliases, i, o = {}, n_in, n_out
-    for m in comms:
-        if getattr(m, "goes_on", False):
-            aliases[i + 1] = o
-        i, o = i + len(m.inputs), o + len(m.outputs)
     results = pl.pallas_call(
         kernel,
         grid=grid,
@@ -376,7 +281,6 @@
         ),
         cost_estimate=pl.CostEstimate(flops=flops, bytes_accessed=1 << 24, transcendentals=0),
         name=name,
-        input_output_aliases=aliases,
     )(*ins, *moved)
     results = list(results)
     mine, results = results[:n_out], results[n_out:]
@@ -495,7 +399,7 @@
 def middle(a, dy, wd, saved, weights, comms, number, extra=None):
     cols, rows = 768, 512
     blocks, tiles, n = FF // cols, TOK // rows, 2 * (FF // cols)
-    lead = 1 if weights else 0
+    lead = 5 if weights else 0
     steps = lead + blocks * tiles + 1
     across = TOK // tiles
 
@@ -553,7 +457,7 @@
 
         @pl.when((t >= 0) & (t < blocks * tiles))
         def _():
-            sub = 256
+            sub = 256 if weights else 512
             w = wd_ref[...].reshape(cols, D)
             for k in range(rows // sub):
                 here = pl.ds(k * sub, sub)
@@ -563,7 +467,7 @@
                     u = dot(left, held[j % 2, 1].reshape(D, cols))
                 else:
                     g, u = ins[0][here, :], ins[1][here, :]
-                da = dot(dy_ref[here, :], w, 1, 1).astype(BF).astype(F32)
+                da = dot(dy_ref[pl.ds(pl.multiple_of(i * rows + k * sub, sub), sub), :], w, 1, 1).astype(BF).astype(F32)
                 sig = jax.nn.sigmoid(g)
                 silu = g * sig
                 if weights:
@@ -581,13 +485,16 @@
             finish(2 * j - 1)
 
         happen(1)
-
-        for m in range(2):
-            if m:
-                happen(2)
-
-            @pl.when((t >= 0) & (t < blocks * tiles) & (i == tiles - 1))
-            def _(m=m):
+        if weights:
+
+            @pl.when((t >= 0) & (t < (blocks - 1) * tiles) & (i == tiles - 1))
+            def _():
+                for load in load_block(arrived, held, loads, j + 1, cols):
+                    load.start()
+
+        @pl.when((t >= 0) & (t < blocks * tiles) & (i == tiles - 1))
+        def _():
+            for m in range(2):
                 u = 2 * j + m
 
                 @pl.when(u > 1)
@@ -599,16 +506,7 @@
                     send[m, k] = term[2 * place(at, k) + 1 - at.c]
                     mine[m, k] = term[2 * place(at, k) + at.c]
                 copy(u).start()
-                if m:
-                    finish(2 * j)
-
-        happen(3)
-        if weights:
-
-            @pl.when((t >= 0) & (t < (blocks - 1) * tiles) & (i == tiles - 1))
-            def _():
-                for load in load_block(arrived, held, loads, j + 1, cols):
-                    load.start()
+            finish(2 * j)
 
         @pl.when(step == steps - 1)
         def _():
@@ -635,7 +533,7 @@
     tile = pl.BlockSpec((rows, cols), lambda s: (block(s)[1], block(s)[0]))
     sems = lambda: pltpu.SemaphoreType.DMA((n,))
     ins = [a, dy, wd] + (list(saved) if saved else [])
-    in_specs = [once((TOK, D), lambda s: (0, 0)), pl.BlockSpec((rows, D), lambda s: (block(s)[1], 0)), pl.BlockSpec((2, 384, D), lambda s: (block(s)[0], 0, 0))]
+    in_specs = [once((TOK, D), lambda s: (0, 0)), once((TOK, D), lambda s: (0, 0)), pl.BlockSpec((2, 384, D), lambda s: (block(s)[0], 0, 0))]
     in_specs += [tile, tile] if saved else []
     scratch = [
         pltpu.VMEM((2, TOK, cols), BF), pltpu.VMEM((8, 160, cols), BF), pltpu.VMEM((2, 4, 160, cols), BF), pltpu.VMEM((2, 4, 160, cols), BF),
@@ -643,10 +541,10 @@
     ] + [sems() for _ in range(6)]
     points = extra
     if weights:
-        comms = [Gather(w, 1, blocks, (1, 2, 3), begun) for w, begun in weights] + comms
+        comms = [Gather(weights[0], 1, blocks), Gather(weights[1], 1, blocks)] + comms
         scratch += [pltpu.VMEM((2, 2, 8, 160, cols), BF), pltpu.SemaphoreType.DMA((2, 2))]
-        when = {1: (0, 4, (4, 2), (4, 3), (4, 3)), 2: (0, (4, 2), 5, 6, 7), 3: ((4, 2), 7, 8, (8, 1), (8, 2))}
-        points = {(m, c, k): when[c][k] for m in range(2) for c in when for k in range(5)}
+        when = ((0, 1, 2, 3, 4), (1, 5, 7, 8, (8, 1)), (5, (8, 1), 9, 10, (12, 1)), ((8, 1), 9, 10, 11, (16, 1)))
+        points = {(m, c, k): when[c][k] for m in range(2) for c in range(blocks) for k in range(5)}
     outs = [shape((2, TOK, FF)), shape((2, 2, 160, FF), F32), shape((2, 2, 160, FF))] + ([shape((TOK, FF))] if weights else [])
     out_specs = [
         pl.BlockSpec((2, rows, cols), lambda s: (0, block(s)[1], block(s)[0])), pl.BlockSpec((2, 1, 160, cols), done), ANY,
@@ -692,11 +590,17 @@
 
     def body(at, step, ins, outs, scratch, landed):
         act_ref, dy_ref = ins
-        kept, to_x, to_y = outs
-        mine, send, recv, *sems = scratch
+        kept, far = outs
+        mine, send, recv, to_x, to_y, *sems = scratch
 
         def copy(t):
             return remote(send.at[t % 2], recv.at[t], sems[0:2], t, at.to_sib)
+
+        def along_x(t):
+            return remote(to_x.at[t], far.at[slots[t][0], pl.ds(0, 192), :], sems[2:4], t, at.to_x)
+
+        def along_y(t):
+            return remote(to_y.at[t // 2], far.at[slots[t][1], pl.ds(192, 192), :], sems[4:6], t, at.to_y)
 
         @pl.when(step > 1)
         def _():
@@ -718,11 +622,13 @@
                 total = mine[...].astype(F32) + recv[t].astype(F32)
                 a, b = total[low], total[high]
                 if flows[t][0]:
-                    to_x[slots[t][0]] = a.astype(BF)
+                    to_x[t] = a.astype(BF)
+                    along_x(t).start()
                 else:
                     kept[1 if flows[t][1] else 0, low, :] = a
                 if flows[t][1]:
-                    to_y[slots[t][1]] = b.astype(BF)
+                    to_y[t // 2] = b.astype(BF)
+                    along_y(t).start()
                 else:
                     kept[1 if flows[t][0] else 0, high, :] = b
 
@@ -730,20 +636,27 @@
         def _():
             copy(n - 2).wait_send()
             copy(n - 1).wait_send()
+            for t in range(n):
+                if flows[t][0]:
+                    along_x(t).wait()
+                if flows[t][1]:
+                    along_y(t).wait()
 
     def now(i):
         at = Place()
         fx, fy = 1 - i // 2, 1 - i % 2
         return 0, (at.x + fx * (1 - 2 * at.x)) * 2 + at.y + fy * (1 - 2 * at.y)
 
-    whole = lambda *dims: pl.BlockSpec(dims, lambda i: (0,) * len(dims))
-    return call(
+    sems = lambda: pltpu.SemaphoreType.DMA((n,))
+    (kept, far), got = call(
         "by_down", body, (n,), [act, dy],
         [pl.BlockSpec((TOK, 768), now), once((TOK, D), lambda i: (0, 0))],
-        [shape((2, 384, D), F32), shape((2, 192, D)), shape((2, 192, D))], [whole(2, 384, D), whole(2, 192, D), whole(2, 192, D)],
-        [pltpu.VMEM((384, D), BF), pltpu.VMEM((2, 384, D), BF), pltpu.VMEM((n, 384, D), BF)] + [pltpu.SemaphoreType.DMA((n,)) for _ in range(2)],
+        [shape((2, 384, D), F32), shape((2, 384, D))], [pl.BlockSpec((2, 384, D), lambda i: (0, 0, 0)), ANY],
+        [pltpu.VMEM((384, D), BF), pltpu.VMEM((2, 384, D), BF), pltpu.VMEM((n, 384, D), BF),
+         pltpu.VMEM((2, 192, D), BF), pltpu.VMEM((2, 192, D), BF)] + [sems() for _ in range(6)],
         comms, number, 2 * TOK * D * FF,
     )
+    return Sum(kept[:, None], far[:, None]), got
 
 
 class Sum:
@@ -771,22 +684,18 @@
     def step(x, dy, w_gate, w_up, w_down):
         x, dy = x[0], dy[0]
         (a0, act0, gate0, up0), ((g0,), (u0,), (d0,)) = gate_up(x, w_gate, w_up, w_down, 0)
-        early = [Gather(w_down, 1, 2), Gather(w_gate, 1, 4, (0,)), Gather(w_up, 1, 4, (0,))]
-        when = {(0, 0, 1): 3, (0, 1, 1): 5, (0, 0, 2): 6, (1, 0, 0): 3, (2, 0, 0): 3, (1, 0, 1): 7, (2, 0, 1): 7, (0, 1, 2): 7}
-        (h1, a1), ((d1,), (g1,), (u1,)) = down(act0, d0, x, early, 1, when)
-        dgu1, s_gu1, (act1,), ((g1,), (u1,)) = middle(a1, dy, d1, None, ((w_gate, g1), (w_up, u1)), [], 2)
-        (kept, *parts), _ = by_down(act1, dy, [], 3)
-        (dh1,), ((got,), (far,)) = by_state(dgu1, g1, u1, h1, dy, [s_gu1.cross(), Spread(*parts)], 4)
-        s_d1 = Sum(kept[:, None], far[:, None])
-        (kept, *parts), ((got_d1,),) = by_down(act0, dh1, [s_d1.cross()], 5)
-        comms = [Chain(kept, *parts), Rise(s_gu1.rise(got)), Rise(s_d1.rise(got_d1))]
-        end_d0 = {(0, c, k): when for c in range(2) for k, when in ((1, 6), (2, 10), (3, 15))}
-        dgu0, s_gu0, _, ((down0,), (z_gu1,), (z_d1,)) = middle(a0, dh1, d0, (gate0, up0), None, comms, 6, end_d0)
+        (h1, a1), ((d1,),) = down(act0, d0, x, [Gather(w_down, 1, 2)], 1, {(0, 0, 1): 3, (0, 1, 1): 6, (0, 0, 2): 7})
+        dgu1, s_gu1, (act1,), ((g1,), (u1,)) = middle(a1, dy, d1, None, (w_gate, w_up), [], 2)
+        s_d1, _ = by_down(act1, dy, [], 3)
+        (dh1,), ((got,), (got_d1,)) = by_state(dgu1, g1, u1, h1, dy, [s_gu1.cross(), s_d1.cross()], 4)
+        s_d0, ((z_d1,),) = by_down(act0, dh1, [Rise(s_d1.rise(got_d1))], 5)
+        end_d0 = {(0, 0, 1): 3, (0, 1, 1): 4, (0, 0, 2): 14, (0, 1, 2): 15}
+        dgu0, s_gu0, _, ((down0,), (z_gu1,)) = middle(a0, dh1, d0, (gate0, up0), None, [s_d0.finish(), Rise(s_gu1.rise(got))], 6, end_d0)
         end_gu0 = {(0, 0, 1): 1, (0, 1, 1): 2, (0, 2, 1): 3, (0, 3, 1): 4, (0, 0, 2): 4, (0, 1, 2): 6, (0, 2, 2): 7}
         (dx,), ((gu0,),) = by_state(dgu0, g0, u0, x, dh1, [s_gu0.finish()], 7, end_gu0)
 
         gu1, down1 = s_gu1.end(z_gu1), s_d1.end(z_d1)
-        return dx[None], jnp.stack([gu0[0], gu1[0]]), jnp.stack([gu0[1], gu1[1]]), jnp.stack([down0, down1[0]])
+        return dx[None], jnp.stack([gu0[0], gu1[0]]), jnp.stack([gu0[1], gu1[1]]), jnp.stack([down0[0], down1[0]])
 
     states, cut = P(("rep", "r", "s"), None, None), P(None, "s", None)
     return jax.shard_map(

time: 637 us -> 637 us (level)
  no operation moved by 1% of the time
where the time goes in v3:
time: 637 us; the launch traced here: 629 us
  Pallas kernels  588 us (92%)
  other arithmetic  33.2 us (5%)
  local copies, waits for them, and re-layouts  7.38 us (1%)
    pallas_call x8, Pallas kernels, call(): pl.pallas_call(kernel, grid=grid, in_specs=list(in_specs) + [ANY] * len(m...  588 us

profile of v3, /device:TPU:0, one launch (start us, length us, event | category | flops | bytes accessed | tf_op | source)
XLA Modules:
  0.0 629.1 jit_solution(3183478647060684908)
XLA Ops:
  0.6 100.9 %gate_up.1 = (bf16[2048,1280]{1,0:T(8,128)(2,1)}, bf16[2048,3072]{1,0:T(8,128)(2,1)}, f32[2048,3072]{1,0:T(8,128)}, f32[2048,3072]{1,0:T(8,128)}, bf16[8,160,307...) custom-call(bf16[2048,1280]{1,0:T(8,128)(2,1)} %bitcast.23, ...), custom_call_target="tpu_custom_call" | custom-call | flops 32212254720 | bytes 16777216 | tf_op jit(solution)/shard_map/gate_up/pallas_call | solution.py:269
  101.6 39.4 %down.1 = (bf16[2048,1280]{1,0:T(8,128)(2,1)}, bf16[2048,1280]{1,0:T(8,128)(2,1)}, bf16[8,384,1280]{2,1,0:T(8,128)(2,1)}) custom-call(bf16[2048,3072]{1,0:T(8,128)(2,1)} %get-tuple-element.36.refs_0_, bf16[8,384,1280]{2,1,0:T(8,128)(2,1)} %get-tuple-element.37.refs_1_.refs_2_, bf16[2048,1280]{1,0:T(8,128)(2,1)} %bitcast.24, bf16[2,384,1280]{2,1,0:T(8,128)(2,1)} %refs_3_.4), custom_call_target="tpu_custom_call" | custom-call | flops 16106127360 | bytes 16777216 | tf_op jit(solution)/shard_map/down/pallas_call | solution.py:269
  141.0 163.4 %middle.2 = (bf16[2,2048,3072]{2,1,0:T(8,128)(2,1)}, f32[2,2,160,3072]{3,2,1,0:T(8,128)}, bf16[2,2,160,3072]{3,2,1,0:T(8,128)(2,1)}, bf16[2048,3072]{1,0:T(8,128...) custom-call(bf16[2048,1280]{1,0:T(8,128)(2,1)} %get-tuple-element.38.refs_0_, ...), custom_call_target="tpu_custom_call" | custom-call | flops 80530636800 | bytes 16777216 | tf_op jit(solution)/shard_map/middle/pallas_call | solution.py:269
  304.4 4.6 fusion.refs_5_
  309.0 35.7 %by_down.2 = (f32[2,384,1280]{2,1,0:T(8,128)}, bf16[2,384,1280]{2,1,0:T(8,128)(2,1)}) custom-call(bf16[2048,3072]{1,0:T(8,128)(2,1)} %get-tuple-element.46.refs_0_, bf16[2048,1280]{1,0:T(8,128)(2,1)} %bitcast.21), custom_call_target="tpu_custom_call" | custom-call | flops 16106127360 | bytes 16777216 | tf_op jit(solution)/shard_map/by_down/pallas_call | solution.py:269
  344.7 2.9 add_convert_fusion.5.refs_6_
  347.7 47.2 %by_state.2 = (bf16[2048,1280]{1,0:T(8,128)(2,1)}, bf16[2,160,3072]{2,1,0:T(8,128)(2,1)}, bf16[1,384,1280]{2,1,0:T(8,128)(2,1)}) custom-call(bf16[2,2048,3072]{2,1,0:T(8,128)(2,1)} %get-tuple-element.40.refs_0_, bf16[8,160,3072]{2,1,0:T(8,128)(2,1)} %get-tuple-element.41.refs_1_, bf16[8,160,3072]{2,1,0:T(8,128)(2,1)} %get-tuple-element.42.refs_2_, ...), custom_call_target="tpu_custom_call" | custom-call | flops 32212254720 | bytes 16777216 | tf_op jit(solution)/shard_map/by_state/pallas_call | solution.py:269
  394.9 3.4 fusion.3.refs_2_
  398.3 36.0 %by_down.3 = (f32[2,384,1280]{2,1,0:T(8,128)}, bf16[2,384,1280]{2,1,0:T(8,128)(2,1)}, bf16[1,384,1280]{2,1,0:T(8,128)(2,1)}) custom-call(bf16[2048,3072]{1,0:T(8,128)(2,1)} %get-tuple-element.36.refs_0_, bf16[2048,1280]{1,0:T(8,128)(2,1)} %get-tuple-element.49.refs_1_.refs_4_, bf16[1,384,1280]{2,1,0:T(8,128)(2,1)} %fusion.3.refs_2_), custom_call_target="tpu_custom_call" | custom-call | flops 16106127360 | bytes 16777216 | tf_op jit(solution)/shard_map/by_down/pallas_call | solution.py:269
  434.3 0.0 copy-done.2
  434.3 0.0 copy-start
  434.3 0.0 copy-start.1
  434.4 5.1 add_convert_fusion.3
  439.5 0.0 copy-done
  439.5 4.4 fusion.2.refs_8_
  443.9 104.6 %middle.3 = (bf16[2,2048,3072]{2,1,0:T(8,128)(2,1)}, f32[2,2,160,3072]{3,2,1,0:T(8,128)}, bf16[2,2,160,3072]{3,2,1,0:T(8,128)(2,1)}, bf16[1,384,1280]{2,1,0:T(8,128)(2,1)}, bf16[2,160,3072]{2,1,0:T(8,128)(2,1)}) custom-call(bf16[2048,1280]{1,0:T(8,128)(2,1)} %get-tuple-element.35.refs_0_, bf16[2048,1280]{1,0:T(8,128)(2,1)} %get-tuple-element.49.refs_1_.refs_4_, ...), custom_call_target="tpu_custom_call" | custom-call | flops 48318382080 | bytes 16777216 | tf_op jit(solution)/shard_map/middle/pallas_call | solution.py:269
  548.5 5.2 add_convert_fusion
  553.7 0.0 copy-start.3
  553.8 1.1 fusion.5
  554.8 0.4 copy-done.3
  555.3 0.3 copy-done.6
  555.6 1.4 pad_maximum_fusion.2
  557.0 1.4 copy-done.5
  558.4 1.9 fusion.1.refs_5_
  560.3 60.2 %by_state.3 = (bf16[2048,1280]{1,0:T(8,128)(2,1)}, bf16[2,160,3072]{2,1,0:T(8,128)(2,1)}) custom-call(bf16[2,2048,3072]{2,1,0:T(8,128)(2,1)} %get-tuple-element.56.refs_0_, bf16[8,160,3072]{2,1,0:T(8,128)(2,1)} %get-tuple-element.57.refs_1_, bf16[8,160,3072]{2,1,0:T(8,128)(2,1)} %get-tuple-element.58.refs_2_, bf16[2048,1280]{1,0:T(8,128)(2,1)} %bitcast.25, ...), custom_call_target="tpu_custom_call" | custom-call | flops 32212254720 | bytes 16777216 | tf_op jit(solution)/shard_map/by_state/pallas_call | solution.py:269
  620.5 0.0 slice-start
  620.5 1.8 fusion.4
  622.3 0.0 slice-start.1
  622.3 2.8 pad_maximum_fusion.1
  625.1 1.4 pad_maximum_fusion
  626.5 0.0 slice-done
  626.5 2.4 copy.10
  (8 shorter events, 0.0 us)
Async XLA Ops:
  398.3 36.0 %copy-start.2 = (bf16[1,384,1280]{2,1,0:T(8,128)(2,1)S(1)}, bf16[1,384,1280]{2,1,0:T(8,128)(2,1)}, u32[]{:S(2)}) copy-start(bf16[1,384,1280]{2,1,0:T(8,128)(2,1)} %get-tuple-element.52) | copy-start | bytes 2949124
  434.3 5.2 copy-start
  434.3 5.1 copy-start.1
  548.5 8.6 %copy-start.4 = (f32[2,2,160,3072]{3,2,1,0:T(8,128)S(1)}, f32[2,2,160,3072]{3,2,1,0:T(8,128)}, u32[]{:S(2)}) copy-start(f32[2,2,160,3072]{3,2,1,0:T(8,128)} %get-tuple-element.59.refs_6_) | copy-start | bytes 23592964
  553.7 1.5 copy-start.3
  553.7 1.8 copy-start.6
  555.6 2.8 copy-start.5
  620.5 6.0 slice-start
  622.3 4.2 slice-start.1
